TPU v7x, 32 devices: a 4x4x1 block of a 4x4x8 slice. The times are simulated.
32 devices in a mesh: dp: 1 (over z), dm: 4 (over y), tp: 8 (over x, core).
Axes of the slice: x: 4, y: 4, z: 1, core: 2. Of those that a mesh axis runs over, the one named last changes fastest.
The devices are a block of a 4x4x8 slice.
Arguments:
- hidden: bfloat16 [256, 5120], P('dp', 'dm')
- w_q: bfloat16 [5120, 40, 128], P('dm', 'tp')
- w_k: bfloat16 [5120, 40, 128], P('dm', 'tp')
- w_v: bfloat16 [5120, 40, 128], P('dm', 'tp')
- w_o: bfloat16 [40, 128, 5120], P('tp', None, 'dm')
- w_gate: bfloat16 [5120, 13824], P('dm', 'tp')
- w_up: bfloat16 [5120, 13824], P('dm', 'tp')
- w_down: bfloat16 [13824, 5120], P('tp', 'dm')
- norm_attn: bfloat16 [5120], P('dm')
- norm_mlp: bfloat16 [5120], P('dm')
- k_cache: bfloat16 [256, 64, 40, 128], P(('dp', 'dm'), None, 'tp')
- v_cache: bfloat16 [256, 64, 40, 128], P(('dp', 'dm'), None, 'tp')
- seq_lens: int32 [256], P(('dp', 'dm'))
- rope_cos: float32 [256, 64], P(('dp', 'dm'))
- rope_sin: float32 [256, 64], P(('dp', 'dm'))
Outputs:
- output 1: bfloat16 [256, 5120], P('dp', 'dm')
- output 2: bfloat16 [256, 64, 40, 128], P(('dp', 'dm'), None, 'tp')
- output 3: bfloat16 [256, 64, 40, 128], P(('dp', 'dm'), None, 'tp')
All inputs are finite; a program needn't handle non-finite values.
Results may differ from a plain program's by a relative error of at most 0.0106647.
Values are sent between devices in bfloat16 or wider.
A program may use at most 768 MiB of HBM per device.

v0:
```python
import jax
import jax.numpy as jnp
from jax import lax
from jax.sharding import PartitionSpec as P

EPS = 1e-6


def width_norm(x, gain, width_full):
    x_f32 = x.astype(jnp.float32)
    sq_sum = lax.psum(jnp.sum(x_f32 * x_f32, axis=-1, keepdims=True), 'dm')
    scale = lax.rsqrt(sq_sum / width_full + EPS)
    return (x_f32 * scale * gain.astype(jnp.float32)).astype(jnp.bfloat16)


def apply_rope(x, rope_cos, rope_sin):
    half = x.shape[-1] // 2
    first = x[..., :half]
    second = x[..., half:]
    cosine = rope_cos[:, None, :]
    sine = rope_sin[:, None, :]
    return jnp.concatenate([first * cosine - second * sine, second * cosine + first * sine], axis=-1).astype(jnp.bfloat16)


def attend(q_rot, k_rot, v_new, k_cache, v_cache, seq_lens):
    rows, seq_len, kv_local, head_dim = k_cache.shape
    positions = jnp.arange(seq_len)
    write_mask = (positions[None, :] == seq_lens[:, None])[:, :, None, None]
    k_out = jnp.where(write_mask, k_rot[:, None], k_cache)
    v_out = jnp.where(write_mask, v_new[:, None], v_cache)
    q_grp = q_rot.reshape(rows, kv_local, -1, head_dim)
    scores = jnp.einsum('bkgd,bskd->bkgs', q_grp, k_out, preferred_element_type=jnp.float32) * (head_dim ** -0.5)
    key_mask = (positions[None, :] <= seq_lens[:, None])[:, None, None, :]
    scores = jnp.where(key_mask, scores, -1e30)
    attn_probs = jax.nn.softmax(scores, axis=-1).astype(jnp.bfloat16)
    heads = jnp.einsum('bkgs,bskd->bkgd', attn_probs, v_out, preferred_element_type=jnp.float32)
    return heads.astype(jnp.bfloat16).reshape(rows, -1, head_dim), k_out, v_out


def solution(mesh):
    width_shards = mesh.shape['dm']
    row_spec = P('dp', 'dm')
    cache_spec = P(('dp', 'dm'), None, 'tp', None)
    batch_spec = P(('dp', 'dm'))
    rope_spec = P(('dp', 'dm'), None)
    in_specs = (row_spec, P('dm', 'tp', None), P('dm', 'tp', None), P('dm', 'tp', None), P('tp', None, 'dm'), P('dm', 'tp'), P('dm', 'tp'), P('tp', 'dm'), P('dm'), P('dm'), cache_spec, cache_spec, batch_spec, rope_spec, rope_spec)
    out_specs = (row_spec, cache_spec, cache_spec)

    def local_layer(hidden, w_q, w_k, w_v, w_o, w_gate, w_up, w_down, norm_attn, norm_mlp, k_cache, v_cache, seq_lens, rope_cos, rope_sin):
        width_full = hidden.shape[1] * width_shards
        x_norm = width_norm(hidden, norm_attn, width_full)
        q_part = jnp.einsum('bd,dhk->bhk', x_norm, w_q, preferred_element_type=jnp.float32)
        k_part = jnp.einsum('bd,dhk->bhk', x_norm, w_k, preferred_element_type=jnp.float32)
        v_part = jnp.einsum('bd,dhk->bhk', x_norm, w_v, preferred_element_type=jnp.float32)
        q_rows = lax.psum_scatter(q_part, 'dm', scatter_dimension=0, tiled=True)
        k_rows = lax.psum_scatter(k_part, 'dm', scatter_dimension=0, tiled=True)
        v_rows = lax.psum_scatter(v_part, 'dm', scatter_dimension=0, tiled=True)
        q_rot = apply_rope(q_rows, rope_cos, rope_sin)
        k_rot = apply_rope(k_rows, rope_cos, rope_sin)
        attn_heads, k_out, v_out = attend(q_rot, k_rot, v_rows.astype(jnp.bfloat16), k_cache, v_cache, seq_lens)
        heads_all = lax.all_gather(attn_heads, 'dm', axis=0, tiled=True)
        attn_part = jnp.einsum('bhk,hkd->bd', heads_all, w_o, preferred_element_type=jnp.float32)
        attn_out = lax.psum(attn_part, 'tp').astype(jnp.bfloat16)
        h_mid = hidden + attn_out
        x_mlp = width_norm(h_mid, norm_mlp, width_full)
        gate = lax.psum(jnp.dot(x_mlp, w_gate, preferred_element_type=jnp.float32), 'dm')
        up_proj = lax.psum(jnp.dot(x_mlp, w_up, preferred_element_type=jnp.float32), 'dm')
        gated_act = (jax.nn.silu(gate) * up_proj).astype(jnp.bfloat16)
        mlp_out = lax.psum(jnp.dot(gated_act, w_down, preferred_element_type=jnp.float32), 'tp').astype(jnp.bfloat16)
        return h_mid + mlp_out, k_out, v_out

    return jax.shard_map(local_layer, mesh=mesh, in_specs=in_specs, out_specs=out_specs, check_vma=False)
```

profile of v0, /device:TPU:97, one launch (start us, length us, event | category | flops | bytes accessed | tf_op | source)
XLA Modules:
  0.0 328.5 jit_solution(11967984775631291363)
XLA Ops:
  7.2 0.0 copy-start
  7.2 0.1 reduce-scatter.8.cloned.1.call-start
  7.3 1.4 fusion.2
  8.7 11.2 %psum.42 = f32[256,1]{0,1:T(1,128)S(1)} all-reduce(f32[256,1]{0,1:T(1,128)S(1)} %bitcast.39), channel_id=1, replica_groups=mesh['dp'=1,'dm'=4,'tp'=8] {'dm'}, use_global_device_ids=true, to_apply=%region_1.0 | all-reduce | flops 256 | bytes 2048 | tf_op jit(solution)/shard_map/psum | solution.py:11
  19.9 0.7 convert_element_type.47
  20.6 3.3 fusion.30
  23.8 0.1 reduce-scatter.8.cloned.1.call-update
  23.9 0.1 reduce-scatter.6.cloned.1.call-start
  24.0 0.0 copy-done.2
  24.0 3.0 fusion.32
  27.0 0.1 reduce-scatter.6.cloned.1.call-update
  27.1 0.0 copy-start.5
  27.1 0.0 copy-start.6
  27.1 0.0 copy-start.3
  27.1 0.0 copy-start.4
  27.1 0.1 reduce-scatter.4.cloned.1.call-start
  27.2 3.0 fusion.34
  30.2 0.1 reduce-scatter.4.cloned.1.call-update
  30.2 0.1 all-reduce.5.cloned.1.call-start
  30.3 0.0 copy-done.5
  30.3 0.0 copy-done.6
  30.3 0.1 iota_compare_fusion.1
  30.4 12.1 %reduce-scatter.8.cloned.1.call-done = f32[64,5,128]{2,0,1:T(8,128)} async-done(((f32[256,5,128]{2,0,1:T(8,128)}), f32[64,5,128]{2,0,1:T(8,128)}) %reduce-scatter.8.cloned.1.call-update) | async-done | bytes 163856 | tf_op jit(solution)/shard_map/reduce_scatter | solution.py:57
  42.5 0.9 convert_element_type.50
  43.4 0.1 copy.23
  43.5 21.1 %reduce-scatter.6.cloned.1.call-done = f32[64,5,128]{2,0,1:T(8,128)} async-done(((f32[256,5,128]{2,0,1:T(8,128)}), f32[64,5,128]{2,0,1:T(8,128)}) %reduce-scatter.6.cloned.1.call-update) | async-done | bytes 163856 | tf_op jit(solution)/shard_map/reduce_scatter | solution.py:56
  64.6 22.2 %reduce-scatter.4.cloned.1.call-done = f32[64,5,128]{2,0,1:T(8,128)} async-done(((f32[256,5,128]{2,0,1:T(8,128)}), f32[64,5,128]{2,0,1:T(8,128)}) %reduce-scatter.4.cloned.1.call-update) | async-done | bytes 163856 | tf_op jit(solution)/shard_map/reduce_scatter | solution.py:55
  86.8 1.3 subtract_convert_fusion.1
  88.1 0.1 pad_maximum_fusion
  88.2 0.1 copy.22
  88.3 0.1 maximum_bitcast_fusion
  88.4 7.4 %broadcast_select_fusion.1 = (bf16[64,64,5,128]{3,1,2,0:T(8,128)(2,1)S(1)}, bf16[64,64,5,128]{3,1,2,0:T(8,128)(2,1)}) fusion(bf16[64,64,5,128]{3,1,2,0:T(8,128)(2,1)} %param.25, pred[64,64]{1,0:T(8,128)(4,1)S(1)} %get-tuple-element.16, bf16[64,5,128]{2,1,0:T(8,128)(2,1)S(1)} %copy.22, bf16[64,64,5,128]{3,1,2,0:T(8,128)(2,1)} %param.26, ...), kind=kLoop, calls=%fused_computation.3 | loop fusion | flops 5242880 | bytes 21139456 | tf_op jit(solution)/shard_map/jit(_where)/select_n | solution.py:29
  95.8 2.8 fusion.23
  98.6 0.2 fusion.12
  98.9 3.9 %fusion.21 = bf16[64,5,1,128]{3,2,1,0:T(2,128)(2,1)S(1)} fusion(bf16[64,64,5,128]{3,1,2,0:T(8,128)(2,1)} %get-tuple-element.14, bf16[64,5,64,1]{2,0,1,3:T(8,128)(2,1)S(1)} %fusion.12), kind=kOutput, calls=%fused_computation.31 | convolution fusion | flops 5242880 | bytes 5365760 | tf_op jit(solution)/shard_map/bkgs,bskd->bkgd/dot_general | solution.py:36
  102.8 10.6 %all_gather.3 = bf16[256,5,128]{2,0,1:T(8,128)(2,1)S(1)} all-gather(bf16[64,5,128]{2,0,1:T(8,128)(2,1)S(1)} %bitcast.37), channel_id=1, replica_groups=mesh['dp'=1,'dm'=4,'tp'=8] {'dm'}, dimensions={0}, use_global_device_ids=true | all-gather | bytes 409600 | tf_op jit(solution)/shard_map/all_gather | solution.py:61
  113.4 0.0 copy-done
  113.4 0.7 convolution_bitcast_fusion
  114.1 54.9 %all-reduce.6 = bf16[256,1280]{1,0:T(8,128)(2,1)} all-reduce(f32[256,1280]{1,0:T(8,128)S(1)} %convolution_bitcast_fusion), channel_id=1, replica_groups=mesh['dp'=1,'dm'=4,'tp'=8] {'tp'}, use_global_device_ids=true, to_apply=%region_7.8 | all-reduce | flops 327680 | bytes 1966080 | tf_op jit(solution)/shard_map/psum | solution.py:63
  169.0 1.6 fusion.5
  170.6 6.8 %psum.44 = f32[256,1]{0,1:T(1,128)S(1)} all-reduce(f32[256,1]{0,1:T(1,128)S(1)} %bitcast.38), channel_id=1, replica_groups=mesh['dp'=1,'dm'=4,'tp'=8] {'dm'}, use_global_device_ids=true, to_apply=%region_9.10 | all-reduce | flops 256 | bytes 2048 | tf_op jit(solution)/shard_map/psum | solution.py:11
  177.4 4.9 %fusion.16 = f32[256,1728]{0,1:T(8,128)} fusion(bf16[1280,1728]{0,1:T(8,128)(2,1)} %param.21, bf16[256,1280]{1,0:T(8,128)(2,1)S(1)} %get-tuple-element.6, f32[1280]{0:T(1024)S(1)} %convert_element_type.54, f32[256]{0:T(256)S(1)} %bitcast.43), kind=kOutput, calls=%fused_computation.26 | convolution fusion | flops 1133772800 | bytes 6854656 | tf_op jit(solution)/shard_map/dot_general | solution.py:67
  182.3 4.9 %fusion.18 = f32[256,1728]{0,1:T(8,128)} fusion(bf16[1280,1728]{0,1:T(8,128)(2,1)} %param.20, bf16[256,1280]{1,0:T(8,128)(2,1)S(1)} %get-tuple-element.6, f32[1280]{0:T(1024)S(1)} %convert_element_type.54, f32[256]{0:T(256)S(1)} %bitcast.44), kind=kOutput, calls=%fused_computation.27 | convolution fusion | flops 1133772800 | bytes 6854656 | tf_op jit(solution)/shard_map/dot_general | solution.py:66
  187.2 0.1 all-reduce.5.cloned.1.call-update
  187.3 76.9 %all-reduce.5.cloned.1.call-done = (f32[256,1728]{0,1:T(8,128)}, f32[256,1728]{0,1:T(8,128)}) async-done(((f32[256,1728]{0,1:T(8,128)}, f32[256,1728]{0,1:T(8,128)}), (f32[256,1728]{0,1:T(8,128)}, f32[256,1728]{0,1:T(8,128)})) %all-reduce.5.cloned.1.call-update) | async-done | bytes 3538960 | tf_op jit(solution)/shard_map/psum | solution.py:67
  264.1 5.8 %fusion.13 = f32[256,1280]{1,0:T(8,128)} fusion(bf16[1728,1280]{1,0:T(8,128)(2,1)} %param.22, f32[256,1728]{0,1:T(8,128)} %get-tuple-element.3, f32[256,1728]{0,1:T(8,128)} %get-tuple-element.4), kind=kOutput, calls=%fused_computation.21 | convolution fusion | flops 1135116288 | bytes 9273344 | tf_op jit(solution)/shard_map/dot_general | solution.py:69
  270.0 51.0 %all-reduce.7 = bf16[256,1280]{1,0:T(8,128)(2,1)S(1)} all-reduce(f32[256,1280]{1,0:T(8,128)} %fusion.13), channel_id=1, replica_groups=mesh['dp'=1,'dm'=4,'tp'=8] {'tp'}, use_global_device_ids=true, to_apply=%region_12.13 | all-reduce | flops 327680 | bytes 1966080 | tf_op jit(solution)/shard_map/psum | solution.py:69
  321.0 1.0 add.55
  (9 shorter events, 0.1 us)
Async XLA Ops:
  7.2 106.2 %copy-start = (bf16[5,128,1280]{2,1,0:T(8,128)(2,1)S(1)}, bf16[5,128,1280]{2,1,0:T(8,128)(2,1)}, u32[]{:S(2)}) copy-start(bf16[5,128,1280]{2,1,0:T(8,128)(2,1)} %param.19) | copy-start | bytes 4915204
  7.2 35.3 %reduce-scatter.8.cloned.1.call-start = ((), (), s32[]{:S(2)}) async-start(), calls=%async_computation.5 | async-start | bytes 819200 | tf_op jit(solution)/shard_map/reduce_scatter | solution.py:57
  20.6 3.4 %copy-start.2 = (bf16[256,1280]{1,0:T(8,128)(2,1)S(1)}, bf16[256,1280]{1,0:T(8,128)(2,1)}, u32[]{:S(2)}) copy-start(bf16[256,1280]{1,0:T(8,128)(2,1)} %param.15) | copy-start | bytes 1966084
  23.9 40.7 %reduce-scatter.6.cloned.1.call-start = ((), (), s32[]{:S(2)}) async-start(), calls=%async_computation.4 | async-start | bytes 819200 | tf_op jit(solution)/shard_map/reduce_scatter | solution.py:56
  27.1 3.3 copy-start.5
  27.1 3.3 copy-start.6
  27.1 59.7 %copy-start.3 = (f32[64,64]{1,0:T(8,128)S(1)}, f32[64,64]{1,0:T(8,128)}, u32[]{:S(2)}) copy-start(f32[64,64]{1,0:T(8,128)} %param.29) | copy-start | bytes 49156
  27.1 59.7 %copy-start.4 = (f32[64,64]{1,0:T(8,128)S(1)}, f32[64,64]{1,0:T(8,128)}, u32[]{:S(2)}) copy-start(f32[64,64]{1,0:T(8,128)} %param.28) | copy-start | bytes 49156
  27.1 59.7 %reduce-scatter.4.cloned.1.call-start = ((), (), s32[]{:S(2)}) async-start(), calls=%async_computation.3 | async-start | bytes 819200 | tf_op jit(solution)/shard_map/reduce_scatter | solution.py:55
  30.2 233.9 %all-reduce.5.cloned.1.call-start = ((), (), s32[]{:S(2)}) async-start(), calls=%async_computation.6 | async-start | bytes 7077888 | tf_op jit(solution)/shard_map/psum | solution.py:67
  95.8 2.8 copy-start.1
Sparse Core Ops, SparseCore 0:
  24.0 18.4 reduce-scatter.7
  45.4 19.2 reduce-scatter.5
  67.5 19.2 reduce-scatter.3
  187.4 76.6 all-reduce.4
where the time goes:
time: 330 us; the launch traced here: 328 us
  blocking collectives  134 us (41%)
  waiting for transfers between devices  132 us (40%)
  matrix products  32.4 us (10%)
  other arithmetic  14.9 us (5%)
  between operations  13.9 us (4%)
    psum x1, waiting for transfers between devices, local_layer(): lax.psum(jnp.dot(x_mlp, w_up, preferred_element_type=jnp.float32), 'dm')  76.9 us
    psum x1, blocking collectives, local_layer(): attn_out = lax.psum(attn_part, 'tp').astype(jnp.bfloat16)  54.9 us
    psum x1, blocking collectives, local_layer(): lax.psum(jnp.dot(gated_act, w_down, preferred_element_type=jnp.float32),...  51 us
    reduce_scatter x1, waiting for transfers between devices, local_layer(): q_rows = lax.psum_scatter(q_part, 'dm', scatter_dimension=0, tiled=True)  22.2 us
    reduce_scatter x1, waiting for transfers between devices, local_layer(): k_rows = lax.psum_scatter(k_part, 'dm', scatter_dimension=0, tiled=True)  21.1 us
    psum x2, blocking collectives, width_norm(): sq_sum = lax.psum(jnp.sum(x_f32 * x_f32, axis=-1, keepdims=True), 'dm')  18 us
    reduce_scatter x1, waiting for transfers between devices, local_layer(): v_rows = lax.psum_scatter(v_part, 'dm', scatter_dimension=0, tiled=True)  12.1 us
    all_gather x1, blocking collectives, local_layer(): heads_all = lax.all_gather(attn_heads, 'dm', axis=0, tiled=True)  10.6 us
  transfers between devices with their start and end apart: 4, of which 4 were waited for; matrix products, arithmetic and copies ran while one was open for 2% of the time, Pallas kernels for 0%

commit v1 on v0

v1 whole, which is shorter than its diff:
```python
import functools

import jax
import jax.numpy as jnp
from jax import lax
from jax.experimental import pallas as pl
from jax.experimental.pallas import tpu as pltpu
from jax.sharding import PartitionSpec as P

EPS = 1e-6
F32 = jnp.float32
BF16 = jnp.bfloat16
MESH = pl.DeviceIdType.MESH
PARTS = 3


def remote(src, dst, send, recv, axis, index):
    return pltpu.make_async_remote_copy(
        src_ref=src, dst_ref=dst, send_sem=send, recv_sem=recv, device_id={axis: index}, device_id_type=MESH)


def entry_barrier(peers):
    barrier = pltpu.get_barrier_semaphore()
    for axis, index in peers:
        pl.semaphore_signal(barrier, inc=1, device_id={axis: index}, device_id_type=MESH)
    return lambda: pl.semaphore_wait(barrier, len(peers))


def column_to_row(col):
    rows = col.shape[0]
    return jnp.concatenate(
        [jnp.broadcast_to(col[i:i + 128], (128, 128)).T[:8] for i in range(0, rows, 128)], axis=1)


def row_to_column(row):
    rows = row.shape[1]
    return jnp.concatenate(
        [jnp.broadcast_to(row[:1, i:i + 128], (128, 128)).T for i in range(0, rows, 128)], axis=0)


def scale_rows(x, scale, gain):
    width = x.shape[1]
    cols = [x[:, i:i + 128] * scale * gain[:, i:i + 128] for i in range(0, width, 128)]
    return jnp.concatenate(cols, axis=1).astype(BF16)


def qkv_kernel(nd, width_full, h_ref, g_ref, cos_ref, sin_ref, wq_hbm, wk_hbm, wv_hbm, q_out, k_out, v_out,
               w_buf, x_buf, part, ss_send, ss_recv, a_recv, b_recv, c_send, c_recv, cos2, sin2,
               w_sem, ss_s, ss_r, a_s, a_r, b_s, b_r, c_s, c_r):
    dm = lax.axis_index('dm')
    nxt, prv, far = lax.rem(dm + 1, nd), lax.rem(dm + nd - 1, nd), lax.rem(dm + 2, nd)
    rows = h_ref.shape[0] // nd
    half = rows // 2
    heads = w_buf.shape[1]

    wait_barrier = entry_barrier([('dm', nxt), ('dm', prv), ('dm', far)])
    loads = [pltpu.make_async_copy(src, w_buf.at[t], w_sem.at[t]) for t, src in enumerate((wq_hbm, wk_hbm, wv_hbm))]
    for load in loads:
        load.start()

    x = h_ref[...].astype(F32)
    ss_send[...] = column_to_row(jnp.sum(x * x, axis=-1, keepdims=True))
    wait_barrier()
    ss = [remote(ss_send, ss_recv.at[i], ss_s.at[i], ss_r.at[i], 'dm', peer) for i, peer in enumerate((nxt, prv, far))]
    for copy in ss:
        copy.start()
    hd = cos_ref.shape[1]
    cos2[:, :hd] = cos_ref[...]
    cos2[:, hd:] = cos_ref[...]
    sin2[:, :hd] = -sin_ref[...]
    sin2[:, hd:] = sin_ref[...]
    for copy in ss:
        copy.wait_recv()
    total = ss_send[...] + ss_recv[0] + ss_recv[1] + ss_recv[2]
    scale = row_to_column(lax.rsqrt(total / width_full + EPS))
    x_buf[...] = scale_rows(h_ref[...].astype(F32), scale, g_ref[...].astype(F32))

    def block(owner, second):
        return pl.ds(pl.multiple_of(owner * rows + second * half, half), half)

    peers = (nxt, prv)
    sends = []
    for t in range(3):
        loads[t].wait()
        for hh in range(heads):
            part[t, :, hh * 128:(hh + 1) * 128] = jnp.dot(x_buf[...], w_buf[t, hh], preferred_element_type=F32)
        for d in range(2):
            sends.append(remote(part.at[t, block(far, d)], a_recv.at[d, t], a_s.at[d, t], a_r.at[d, t], 'dm', peers[d]))
            sends[-1].start()
        for d in range(2):
            sends.append(remote(part.at[t, block(peers[d], 1 - d)], b_recv.at[d, t], b_s.at[d, t], b_r.at[d, t], 'dm', peers[d]))
            sends[-1].start()
    for t in range(3):
        for d in range(2):
            remote(a_recv.at[d, t], a_recv.at[d, t], a_s.at[d, t], a_r.at[d, t], 'dm', peers[d]).wait_recv()
            c_send[d, t] = a_recv[d, t] + part[t, block(peers[d], d)]
            sends.append(remote(c_send.at[d, t], c_recv.at[d, t], c_s.at[d, t], c_r.at[d, t], 'dm', peers[d]))
            sends[-1].start()
    for t, out in enumerate((q_out, k_out, v_out)):
        for d in range(2):
            remote(b_recv.at[d, t], b_recv.at[d, t], b_s.at[d, t], b_r.at[d, t], 'dm', peers[d]).wait_recv()
            remote(c_recv.at[d, t], c_recv.at[d, t], c_s.at[d, t], c_r.at[d, t], 'dm', peers[d]).wait_recv()
        for d in range(2):
            tot = part[t, block(dm, d)] + c_recv[d, t] + b_recv[1 - d, t]
            for hh in range(heads):
                y = tot[:, hh * 128:(hh + 1) * 128]
                if t < 2:
                    here = slice(d * half, (d + 1) * half)
                    y = y * cos2[here] + pltpu.roll(y, 64, 1) * sin2[here]
                out[d * half:(d + 1) * half, hh * 128:(hh + 1) * 128] = y.astype(BF16).astype(F32)
    for copy in ss + sends:
        copy.wait_send()


def qkv(nd, hidden, g, cos, sin, wq, wk, wv):
    batch, width = hidden.shape
    heads, _, head = wq.shape
    rows, cols = batch // nd, heads * head
    half = rows // 2
    vmem = pl.BlockSpec(memory_space=pltpu.VMEM)
    hbm = pl.BlockSpec(memory_space=pl.ANY)
    dma = pltpu.SemaphoreType.DMA
    piece = pltpu.VMEM((2, 3, half, cols), F32)
    return pl.pallas_call(
        functools.partial(qkv_kernel, nd, width * nd),
        out_shape=[jax.ShapeDtypeStruct((rows, cols), F32)] * 3,
        in_specs=[vmem] * 4 + [hbm] * 3,
        out_specs=[vmem] * 3,
        scratch_shapes=[
            pltpu.VMEM((3, heads, width, head), BF16), pltpu.VMEM((batch, width), BF16), pltpu.VMEM((3, batch, cols), F32),
            pltpu.VMEM((8, batch), F32), pltpu.VMEM((3, 8, batch), F32), piece, piece, piece, piece,
            pltpu.VMEM((rows, head), F32), pltpu.VMEM((rows, head), F32),
            dma((3,)), dma((3,)), dma((3,))] + [dma((2, 3))] * 6,
        compiler_params=pltpu.CompilerParams(collective_id=0, has_side_effects=True, vmem_limit_bytes=40 * 2 ** 20),
        name='qkv',
    )(hidden, g, cos, sin, wq, wk, wv)


def attend_kernel(lens_ref, q_ref, kn_ref, vn_ref, kc_ref, vc_ref, ko_ref, vo_ref, o_ref):
    step = pl.program_id(0)
    rb, heads, slots, head = kc_ref.shape
    pos = lax.broadcasted_iota(jnp.int32, (heads, slots, head), 1)
    head_row = lax.broadcasted_iota(jnp.int32, (8, heads * slots), 0)
    lane = lax.broadcasted_iota(jnp.int32, (8, heads * slots), 1)
    lane_slot = lane % slots
    own_head = (lane // slots) == head_row
    q_row = lax.broadcasted_iota(jnp.int32, (8, head), 0)
    q_all, kn_all, vn_all = q_ref[...], kn_ref[...], vn_ref[...]
    for r in range(rb):
        length = lens_ref[step * rb + r]
        write = pos == length

        def new(vals):
            return jnp.stack([jnp.broadcast_to(vals[r:r + 1, i * head:(i + 1) * head], (slots, head)) for i in range(heads)])

        k = jnp.where(write, new(kn_all), kc_ref[r].astype(F32)).astype(BF16)
        v = jnp.where(write, new(vn_all), vc_ref[r].astype(F32)).astype(BF16)
        ko_ref[r] = k
        vo_ref[r] = v
        q = jnp.zeros((8, head), F32)
        for i in range(heads):
            q = jnp.where(q_row == i, jnp.broadcast_to(q_all[r:r + 1, i * head:(i + 1) * head], (8, head)), q)
        s = lax.dot_general(q.astype(BF16), k.reshape(heads * slots, head), (((1,), (1,)), ((), ())), preferred_element_type=F32)
        s = jnp.where(own_head & (lane_slot <= length), s * (head ** -0.5), float(jnp.finfo(F32).min))
        p = jnp.exp(s - jnp.max(s, axis=-1, keepdims=True))
        p = jnp.where(own_head & (lane_slot <= length), p, 0.0)
        p = (p / jnp.maximum(jnp.sum(p, axis=-1, keepdims=True), 1e-30)).astype(BF16)
        o = jnp.dot(p, v.reshape(heads * slots, head), preferred_element_type=F32)
        for i in range(heads):
            o_ref[r:r + 1, i * head:(i + 1) * head] = o[i:i + 1]


def attend(lens, q, kn, vn, kc, vc):
    rows, heads, slots, head = kc.shape
    rb = 8
    row_block = pl.BlockSpec((rb, heads * head), lambda i, lens: (i, 0))
    cache_block = pl.BlockSpec((rb, heads, slots, head), lambda i, lens: (i, 0, 0, 0))
    return pl.pallas_call(
        attend_kernel,
        grid_spec=pltpu.PrefetchScalarGridSpec(
            num_scalar_prefetch=1, grid=(rows // rb,),
            in_specs=[row_block] * 3 + [cache_block] * 2,
            out_specs=[cache_block, cache_block, row_block]),
        out_shape=[jax.ShapeDtypeStruct(kc.shape, BF16), jax.ShapeDtypeStruct(vc.shape, BF16),
                   jax.ShapeDtypeStruct((rows, heads * head), F32)],
        compiler_params=pltpu.CompilerParams(vmem_limit_bytes=40 * 2 ** 20),
        name='attend',
    )(lens, q, kn, vn, kc, vc)


def mlp_kernel(nd, nx, width_full, o_ref, h_ref, g_ref, wo_hbm, wg_hbm, wu_hbm, wd_hbm, out_ref,
               wo, wg, wu, wd, o_all, part, d2d_recv, xa_recv, xb_recv, xc_send, xc_recv, h1_buf, ss_send, ss_recv,
               x2_all, gu, ga_recv, gb_recv, gc_send, gc_recv, m_all, h_all,
               w_sem, o_s, o_r, d_s, d_r, xa_s, xa_r, xb_s, xb_r, xc_s, xc_r, ss_s, ss_r,
               ag_s, ag_r, agf_s, agf_r, agd_s, agd_r, ga_s, ga_r, gb_s, gb_r, gc_s, gc_r, m_s, m_r, mf_s, mf_r):
    dm, tp = lax.axis_index('dm'), lax.axis_index('tp')
    nxt, prv, far = lax.rem(dm + 1, nd), lax.rem(dm + nd - 1, nd), lax.rem(dm + 2, nd)
    core, xi = lax.rem(tp, 2), tp // 2
    xn, xp, xf = lax.rem(xi + 1, nx), lax.rem(xi + nx - 1, nx), lax.rem(xi + 2, nx)
    partner = tp + 1 - 2 * core
    ypeers, xpeers, xpeer_ids = (nxt, prv), (xn, xp), (2 * xn + core, 2 * xp + core)
    batch, width = h_ref.shape
    rows = batch // nd
    share = batch // (2 * nx)
    xhalf = share // 2
    cols = wd.shape[0]
    own_cols = cols // nd
    pc = own_cols // PARTS
    ph = pc // 2
    sends = []

    def go(*args):
        sends.append(remote(*args))
        sends[-1].start()

    def got(ref, send, recv, axis, index):
        remote(ref, ref, send, recv, axis, index).wait_recv()

    wait_barrier = entry_barrier([('dm', nxt), ('dm', prv), ('dm', far), ('tp', partner), ('tp', xpeer_ids[0]), ('tp', xpeer_ids[1])])
    loads = [pltpu.make_async_copy(src, dst, w_sem.at[i])
             for i, (src, dst) in enumerate(((wo_hbm, wo), (wg_hbm, wg), (wu_hbm, wu), (wd_hbm, wd)))]
    for load in loads:
        load.start()

    def rows_of(owner, offset=0, count=rows):
        return pl.ds(pl.multiple_of(owner * rows + offset, 16), count)

    o_all[rows_of(dm)] = o_ref[...].astype(BF16)
    wait_barrier()
    for d in range(2):
        mine = o_all.at[rows_of(dm)]
        go(mine, mine, o_s.at[0, d], o_r.at[0, d], 'dm', ypeers[d])
    for d in range(2):
        near = o_all.at[rows_of(ypeers[1 - d])]
        got(near, o_s.at[0, d], o_r.at[0, d], 'dm', ypeers[d])
        piece = o_all.at[rows_of(ypeers[1 - d], d * (rows // 2), rows // 2)]
        go(piece, piece, o_s.at[1, d], o_r.at[1, d], 'dm', ypeers[d])
    for d in range(2):
        got(o_all.at[rows_of(far, d * (rows // 2), rows // 2)], o_s.at[1, d], o_r.at[1, d], 'dm', ypeers[d])

    def tile_rows(owner, c, offset=0, count=share):
        return pl.ds(pl.multiple_of(c * (batch // 2) + owner * share + offset, xhalf), count)

    def tp_scatter(u):
        order = (xf, xn, xp, xi)
        for i, owner in enumerate(order):
            go(part.at[u, tile_rows(owner, 1 - core)], d2d_recv.at[u, i], d_s.at[u, i], d_r.at[u, i], 'tp', partner)
        for i, owner in enumerate(order):
            got(d2d_recv.at[u, i], d_s.at[u, i], d_r.at[u, i], 'tp', partner)
            here = tile_rows(owner, core)
            part[u, here] = part[u, here] + d2d_recv[u, i]
            if i == 0:
                for d in range(2):
                    go(part.at[u, tile_rows(xf, core, d * xhalf, xhalf)], xa_recv.at[u, d], xa_s.at[u, d], xa_r.at[u, d], 'tp', xpeer_ids[d])
            elif i < 3:
                d = i - 1
                go(part.at[u, tile_rows(owner, core, (1 - d) * xhalf, xhalf)], xb_recv.at[u, d], xb_s.at[u, d], xb_r.at[u, d], 'tp', xpeer_ids[d])
        for d in range(2):
            got(xa_recv.at[u, d], xa_s.at[u, d], xa_r.at[u, d], 'tp', xpeer_ids[d])
            xc_send[u, d] = xa_recv[u, d] + part[u, tile_rows(xpeers[d], core, d * xhalf, xhalf)]
            go(xc_send.at[u, d], xc_recv.at[u, d], xc_s.at[u, d], xc_r.at[u, d], 'tp', xpeer_ids[d])
        for d in range(2):
            got(xb_recv.at[u, d], xb_s.at[u, d], xb_r.at[u, d], 'tp', xpeer_ids[d])
            got(xc_recv.at[u, d], xc_s.at[u, d], xc_r.at[u, d], 'tp', xpeer_ids[d])
        return jnp.concatenate(
            [part[u, tile_rows(xi, core, d * xhalf, xhalf)] + xc_recv[u, d] + xb_recv[u, 1 - d] for d in range(2)], axis=0)

    def tp_gather(u, buf):
        mine = buf.at[tile_rows(xi, core)]
        for d in range(2):
            go(mine, mine, ag_s.at[u, d], ag_r.at[u, d], 'tp', xpeer_ids[d])
        go(mine, mine, agd_s.at[u, 0], agd_r.at[u, 0], 'tp', partner)
        for d in range(2):
            near = buf.at[tile_rows(xpeers[1 - d], core)]
            got(near, ag_s.at[u, d], ag_r.at[u, d], 'tp', xpeer_ids[d])
            piece = buf.at[tile_rows(xpeers[1 - d], core, d * xhalf, xhalf)]
            go(piece, piece, agf_s.at[u, d], agf_r.at[u, d], 'tp', xpeer_ids[d])
            go(near, near, agd_s.at[u, 1 + d], agd_r.at[u, 1 + d], 'tp', partner)
        for d in range(2):
            got(buf.at[tile_rows(xf, core, d * xhalf, xhalf)], agf_s.at[u, d], agf_r.at[u, d], 'tp', xpeer_ids[d])
        faraway = buf.at[tile_rows(xf, core)]
        go(faraway, faraway, agd_s.at[u, 3], agd_r.at[u, 3], 'tp', partner)
        for i, owner in enumerate((xi, xp, xn, xf)):
            got(buf.at[tile_rows(owner, 1 - core)], agd_s.at[u, i], agd_r.at[u, i], 'tp', partner)

    loads[0].wait()
    step = 256
    for n in range(0, width, step):
        part[0, :, n:n + step] = jnp.dot(o_all[...], wo[:, n:n + step], preferred_element_type=F32)
    attn = tp_scatter(0)
    h1 = (h_ref[tile_rows(xi, core)] + attn.astype(BF16))
    h1_buf[...] = h1
    h1 = h1.astype(F32)
    col = jnp.sum(h1 * h1, axis=-1, keepdims=True)
    ss_send[...] = column_to_row(jnp.concatenate([col] * (128 // share), axis=0))
    for i, peer in enumerate((nxt, prv, far)):
        go(ss_send, ss_recv.at[i], ss_s.at[i], ss_r.at[i], 'dm', peer)
    for i, peer in enumerate((nxt, prv, far)):
        got(ss_recv.at[i], ss_s.at[i], ss_r.at[i], 'dm', peer)
    total = ss_send[...] + ss_recv[0] + ss_recv[1] + ss_recv[2]
    scale = row_to_column(lax.rsqrt(total / width_full + EPS))[:share]
    x2_all[tile_rows(xi, core)] = scale_rows(h1, scale, g_ref[...].astype(F32))
    tp_gather(0, x2_all)

    loads[1].wait()
    loads[2].wait()

    def columns(owner):
        return pl.ds(pl.multiple_of(owner * own_cols, 16), own_cols)

    for i, owner in enumerate((far, nxt, prv, dm)):
        for j, w in enumerate((wg, wu)):
            y = lax.dot_general(w[columns(owner)], x2_all[...], (((1,), (1,)), ((), ())), preferred_element_type=F32)
            for p in range(PARTS):
                for s in range(2):
                    gu[i, p, s, j] = y[p * pc + s * ph:p * pc + (s + 1) * ph]
        for p in range(PARTS):
            if i == 0:
                for d in range(2):
                    go(gu.at[0, p, d], ga_recv.at[d, p], ga_s.at[d, p], ga_r.at[d, p], 'dm', ypeers[d])
            elif i < 3:
                d = i - 1
                go(gu.at[i, p, 1 - d], gb_recv.at[d, p], gb_s.at[d, p], gb_r.at[d, p], 'dm', ypeers[d])
    for p in range(PARTS):
        for d in range(2):
            got(ga_recv.at[d, p], ga_s.at[d, p], ga_r.at[d, p], 'dm', ypeers[d])
            gc_send[d, p] = ga_recv[d, p] + gu[1 + d, p, d]
            go(gc_send.at[d, p], gc_recv.at[d, p], gc_s.at[d, p], gc_r.at[d, p], 'dm', ypeers[d])

    cut = (pc // 2 + 15) // 16 * 16
    cuts = ((0, cut), (cut, pc - cut))

    def m_rows(owner, p, offset=0, count=pc):
        return pl.ds(pl.multiple_of(owner * own_cols + p * pc + offset, 16), count)

    for p in range(PARTS):
        halves = []
        for d in range(2):
            got(gb_recv.at[d, p], gb_s.at[d, p], gb_r.at[d, p], 'dm', ypeers[d])
            got(gc_recv.at[d, p], gc_s.at[d, p], gc_r.at[d, p], 'dm', ypeers[d])
        for d in range(2):
            gate, up = (gu[3, p, d, j] + gc_recv[d, p, j] + gb_recv[1 - d, p, j] for j in range(2))
            halves.append(gate * jax.nn.sigmoid(gate) * up)
        m_all[m_rows(dm, p)] = jnp.concatenate(halves, axis=0).astype(BF16)
        for d in range(2):
            mine = m_all.at[m_rows(dm, p)]
            go(mine, mine, m_s.at[d, p], m_r.at[d, p], 'dm', ypeers[d])
    for p in range(PARTS):
        for d in range(2):
            got(m_all.at[m_rows(ypeers[1 - d], p)], m_s.at[d, p], m_r.at[d, p], 'dm', ypeers[d])
            piece = m_all.at[m_rows(ypeers[1 - d], p, *cuts[d])]
            go(piece, piece, mf_s.at[d, p], mf_r.at[d, p], 'dm', ypeers[d])
    for p in range(PARTS):
        for d in range(2):
            got(m_all.at[m_rows(far, p, *cuts[d])], mf_s.at[d, p], mf_r.at[d, p], 'dm', ypeers[d])

    loads[3].wait()
    for n in range(0, width, step):
        part[1, :, n:n + step] = lax.dot_general(m_all[...], wd[:, n:n + step], (((0,), (0,)), ((), ())), preferred_element_type=F32)
    mlp = tp_scatter(1)
    h_all[tile_rows(xi, core)] = h1_buf[...] + mlp.astype(BF16)
    tp_gather(1, h_all)
    out_ref[...] = h_all[...]
    for copy in sends:
        copy.wait_send()


def mlp(nd, nx, o, hidden, g, wo, wg, wu, wd):
    batch, width = hidden.shape
    cols = wd.shape[0]
    inner = wo.shape[0]
    share = batch // (2 * nx)
    vmem = pl.BlockSpec(memory_space=pltpu.VMEM)
    hbm = pl.BlockSpec(memory_space=pl.ANY)
    dma = pltpu.SemaphoreType.DMA
    xpiece = pltpu.VMEM((2, 2, share // 2, width), F32)
    ph = cols // nd // PARTS // 2
    gpiece = pltpu.VMEM((2, PARTS, 2, ph, batch), F32)
    return pl.pallas_call(
        functools.partial(mlp_kernel, nd, nx, width * nd),
        out_shape=jax.ShapeDtypeStruct((batch, width), BF16),
        in_specs=[vmem] * 3 + [hbm] * 4,
        out_specs=vmem,
        scratch_shapes=[
            pltpu.VMEM(wo.shape, BF16), pltpu.VMEM(wg.shape, BF16), pltpu.VMEM(wu.shape, BF16), pltpu.VMEM(wd.shape, BF16),
            pltpu.VMEM((batch, inner), BF16), pltpu.VMEM((2, batch, width), F32), pltpu.VMEM((2, nx, share, width), F32),
            xpiece, xpiece, xpiece, xpiece, pltpu.VMEM((share, width), BF16), pltpu.VMEM((8, 128), F32), pltpu.VMEM((3, 8, 128), F32),
            pltpu.VMEM((batch, width), BF16), pltpu.VMEM((4, PARTS, 2, 2, ph, batch), F32), gpiece, gpiece, gpiece, gpiece,
            pltpu.VMEM((cols, batch), BF16), pltpu.VMEM((batch, width), BF16),
            dma((4,)), dma((2, 2)), dma((2, 2)), dma((2, 4)), dma((2, 4))] + [dma((2, 2))] * 6 + [dma((3,))] * 2
        + [dma((2, 2))] * 4 + [dma((2, 4))] * 2 + [dma((2, PARTS))] * 10,
        compiler_params=pltpu.CompilerParams(collective_id=1, has_side_effects=True, vmem_limit_bytes=56 * 2 ** 20),
        name='mlp',
    )(o, hidden, g, wo, wg, wu, wd)


def solution(mesh):
    nd, nx = mesh.shape['dm'], mesh.shape['tp'] // 2
    row_spec = P('dp', 'dm')
    cache_spec = P(('dp', 'dm'), None, 'tp', None)
    batch_spec = P(('dp', 'dm'))
    rope_spec = P(('dp', 'dm'), None)
    in_specs = (row_spec, P('dm', 'tp', None), P('dm', 'tp', None), P('dm', 'tp', None), P('tp', None, 'dm'), P('dm', 'tp'), P('dm', 'tp'), P('tp', 'dm'), P('dm'), P('dm'), cache_spec, cache_spec, batch_spec, rope_spec, rope_spec)
    out_specs = (row_spec, cache_spec, cache_spec)

    def local_layer(hidden, w_q, w_k, w_v, w_o, w_gate, w_up, w_down, norm_attn, norm_mlp, k_cache, v_cache, seq_lens, rope_cos, rope_sin):
        wq, wk, wv = (w.transpose(1, 0, 2) for w in (w_q, w_k, w_v))
        q, kn, vn = qkv(nd, hidden, norm_attn[None, :], rope_cos, rope_sin, wq, wk, wv)
        ko, vo, o = attend(seq_lens, q, kn, vn, k_cache.transpose(0, 2, 1, 3), v_cache.transpose(0, 2, 1, 3))
        h_out = mlp(nd, nx, o, hidden, norm_mlp[None, :], w_o.reshape(-1, w_o.shape[-1]), w_gate.T, w_up.T, w_down)
        return h_out, ko.transpose(0, 2, 1, 3), vo.transpose(0, 2, 1, 3)

    return jax.shard_map(local_layer, mesh=mesh, in_specs=in_specs, out_specs=out_specs, check_vma=False)
```

time: 330 us -> 160 us (0.48)
  Pallas kernels: 0 us -> 144 us
  blocking collectives: 134 us -> 0 us
  waiting for transfers between devices: 132 us -> 0 us
  matrix products: 32.4 us -> 0 us
  other arithmetic: 14.9 us -> 0 us
  local copies, waits for them, and re-layouts: 0.19 us -> 14.3 us
  between operations: 13.9 us -> 0.69 us
    pallas_call x0 -> x3, Pallas kernels: none -> 144 us  [the longest x1 95.2 us: mlp(): pl.pallas_call(functools.partial(mlp_kernel, nd, nx, width * nd), out_sha...]
    psum x4 -> x0, blocking collectives: 124 us -> none  [the longest x1 54.9 us: local_layer(): attn_out = lax.psum(attn_part, 'tp').astype(jnp.bfloat16)]
    psum x1 -> x0, waiting for transfers between devices: 76.9 us -> none  [local_layer(): lax.psum(jnp.dot(x_mlp, w_up, preferred_element_type=jnp.float32), 'dm')]
    reduce_scatter x3 -> x0, waiting for transfers between devices: 55.4 us -> none  [the longest x1 22.2 us: local_layer(): q_rows = lax.psum_scatter(q_part, 'dm', scatter_dimension=0, tiled=True)]
    dot_general x9 -> x0, matrix products: 32.4 us -> none  [the longest x1 5.84 us: local_layer(): jnp.dot(gated_act, w_down, preferred_element_type=jnp.float32)]
    unnamed x14 -> x21, local copies, waits for them, and re-layouts: 0.04 us -> 12 us
    all_gather x1 -> x0, blocking collectives: 10.6 us -> none  [local_layer(): heads_all = lax.all_gather(attn_heads, 'dm', axis=0, tiled=True)]
    select_n x1 -> x0, other arithmetic: 7.41 us -> none  [attend(): k_out = jnp.where(write_mask, k_rot[:, None], k_cache)]
  transfers between devices with their start and end apart: 4 -> 0, of which waited for: 4 -> 0; matrix products, arithmetic and copies ran while one was open for 2% -> 0% of each run, Pallas kernels for 0% -> 0%
where the time goes in v1:
time: 160 us; the launch traced here: 159 us
  Pallas kernels  144 us (90%)
  local copies, waits for them, and re-layouts  14.3 us (9%)
    pallas_call x1, Pallas kernels, mlp(): pl.pallas_call(functools.partial(mlp_kernel, nd, nx, width * nd), out_sha...  95.2 us
    pallas_call x1, Pallas kernels, qkv(): pl.pallas_call(functools.partial(qkv_kernel, nd, width * nd), out_shape=[...  26.1 us
    pallas_call x1, Pallas kernels, attend(): pl.pallas_call(attend_kernel, grid_spec=pltpu.PrefetchScalarGridSpec(num_...  23 us
    unnamed x21, local copies, waits for them, and re-layouts  12 us

profile of v1, /device:TPU:97, one launch (start us, length us, event | category | flops | bytes accessed | tf_op | source)
XLA Modules:
  0.0 159.3 jit_solution(4081514423296309326)
XLA Ops:
  0.6 0.0 copy-start
  0.6 0.8 broadcast_in_dim.6.g_ref
  1.5 1.4 broadcast_in_dim.7.g_ref
  2.9 0.0 copy-start.2
  2.9 1.1 copy-done.2
  4.0 0.0 copy-start.3
  4.0 1.4 copy-done.3
  5.4 0.0 copy-start.4
  5.4 1.4 copy-done.4
  6.9 0.0 copy-start.5
  6.9 1.4 copy-done.5
  8.3 0.0 copy-start.7
  8.3 0.8 copy-done.7
  9.1 0.0 copy-start.8
  9.1 0.8 copy-done.8
  9.8 0.0 copy-start.9
  9.8 26.1 %qkv.1 = (f32[64,640]{1,0:T(8,128)S(1)}, f32[64,640]{1,0:T(8,128)S(1)}, f32[64,640]{1,0:T(8,128)S(1)}) custom-call(bf16[256,1280]{1,0:T(8,128)(2,1)S(1)} %copy-done.2, bf16[1,1280]{1,0:T(2,128)(2,1)S(1)} %broadcast_in_dim.6.g_ref, f32[64,64]{1,0:T(8,128)S(1)} %copy-done.7, f32[64,64]{1,0:T(8,128)S(1)} %copy-done.8, bf16[5,1280,128]{2,1,0:T(8,128)(2,1)S(1)} %bitcast.12, ...), custom_call_target="tpu_custom_call" | custom-call | tf_op jit(solution)/shard_map/qkv/pallas_call | solution.py:124
  35.9 0.0 copy-done
  35.9 0.0 copy-done.9
  35.9 0.0 copy-start.1
  36.0 2.5 %copy-done.1 = bf16[64,64,5,128]{3,1,2,0:T(8,128)(2,1)S(1)} copy-done((bf16[64,64,5,128]{3,1,2,0:T(8,128)(2,1)S(1)}, bf16[64,64,5,128]{3,1,2,0:T(8,128)(2,1)}, u32[]{:S(2)}) %copy-start.1) | copy-done | bytes 5242904
  38.4 23.0 %attend.1 = (bf16[64,5,64,128]{3,2,1,0:T(8,128)(2,1)}, bf16[64,5,64,128]{3,2,1,0:T(8,128)(2,1)}, f32[64,640]{1,0:T(8,128)S(1)}) custom-call(s32[64]{0:T(128)S(1)} %copy-done.9, f32[64,640]{1,0:T(8,128)S(1)} %get-tuple-element.9.q_ref, f32[64,640]{1,0:T(8,128)S(1)} %get-tuple-element.10.kn_ref, f32[64,640]{1,0:T(8,128)S(1)} %get-tuple-element.11.vn_ref, ...), custom_call_target="tpu_custom_call" | custom-call | tf_op jit(solution)/shard_map/attend/pallas_call | solution.py:178
  61.4 0.0 copy-start.6
  61.4 0.7 copy-done.6
  62.1 95.2 %mlp.1 = bf16[256,1280]{1,0:T(8,128)(2,1)} custom-call(f32[64,640]{1,0:T(8,128)} %copy-done.6, bf16[256,1280]{1,0:T(8,128)(2,1)} %h_ref.3, bf16[1,1280]{1,0:T(2,128)(2,1)} %broadcast_in_dim.7.g_ref, bf16[640,1280]{1,0:T(8,128)(2,1)} %bitcast.17, bf16[1728,1280]{1,0:T(8,128)(2,1)} %bitcast.15, bf16[1728,1280]{1,0:T(8,128)(2,1)} %bitcast.16, ...), custom_call_target="tpu_custom_call" | custom-call | tf_op jit(solution)/shard_map/mlp/pallas_call | solution.py:379
  157.4 2.0 %copy.19 = bf16[256,1280]{1,0:T(8,128)(2,1)} copy(bf16[256,1280]{1,0:T(8,128)(2,1)} %mlp.1) | data formatting | bytes 1310720
Async XLA Ops:
  0.6 35.3 %copy-start = (bf16[64,64,5,128]{3,1,2,0:T(8,128)(2,1)S(1)}, bf16[64,64,5,128]{3,1,2,0:T(8,128)(2,1)}, u32[]{:S(2)}) copy-start(bf16[64,64,5,128]{3,1,2,0:T(8,128)(2,1)} %param.25) | copy-start | bytes 15728644
  2.9 1.1 copy-start.2
  4.0 1.4 copy-start.3
  5.4 1.4 copy-start.4
  6.9 1.4 copy-start.5
  8.3 0.8 copy-start.7
  9.1 0.8 copy-start.8
  9.8 26.1 %copy-start.9 = (s32[64]{0:T(128)S(1)}, s32[64]{0:T(128)}, u32[]{:S(2)}) copy-start(s32[64]{0:T(128)} %lens_ref.1) | copy-start | bytes 772
  35.9 2.5 %copy-start.1 = (bf16[64,64,5,128]{3,1,2,0:T(8,128)(2,1)S(1)}, bf16[64,64,5,128]{3,1,2,0:T(8,128)(2,1)}, u32[]{:S(2)}) copy-start(bf16[64,64,5,128]{3,1,2,0:T(8,128)(2,1)} %param.26) | copy-start | bytes 15728644
  61.4 0.7 copy-start.6

commit v2 on v1

--- a/solution.py
+++ b/solution.py
@@ -11,6 +11,7 @@
 F32 = jnp.float32
 BF16 = jnp.bfloat16
 MESH = pl.DeviceIdType.MESH
+VMEM_LIMIT = 63 * 2 ** 20
 PARTS = 3
 
 
@@ -44,9 +45,9 @@
     return jnp.concatenate(cols, axis=1).astype(BF16)
 
 
-def qkv_kernel(nd, width_full, h_ref, g_ref, cos_ref, sin_ref, wq_hbm, wk_hbm, wv_hbm, q_out, k_out, v_out,
-               w_buf, x_buf, part, ss_send, ss_recv, a_recv, b_recv, c_send, c_recv, cos2, sin2,
-               w_sem, ss_s, ss_r, a_s, a_r, b_s, b_r, c_s, c_r):
+def qkv_kernel(nd, width_full, h_hbm, g_hbm, cos_hbm, sin_hbm, wq_hbm, wk_hbm, wv_hbm, q_out, k_out, v_out,
+               h_ref, g_ref, cos_ref, sin_ref, w_buf, x_buf, part, ss_send, ss_recv, a_recv, b_recv, c_send, c_recv, cos2, sin2,
+               in_sem, w_sem, ss_s, ss_r, a_s, a_r, b_s, b_r, c_s, c_r):
     dm = lax.axis_index('dm')
     nxt, prv, far = lax.rem(dm + 1, nd), lax.rem(dm + nd - 1, nd), lax.rem(dm + 2, nd)
     rows = h_ref.shape[0] // nd
@@ -54,16 +55,21 @@
     heads = w_buf.shape[1]
 
     wait_barrier = entry_barrier([('dm', nxt), ('dm', prv), ('dm', far)])
+    small = [pltpu.make_async_copy(src, dst, in_sem.at[i]) for i, (src, dst) in enumerate(
+        ((h_hbm, h_ref), (g_hbm, g_ref), (cos_hbm, cos_ref), (sin_hbm, sin_ref)))]
     loads = [pltpu.make_async_copy(src, w_buf.at[t], w_sem.at[t]) for t, src in enumerate((wq_hbm, wk_hbm, wv_hbm))]
-    for load in loads:
+    for load in small + loads:
         load.start()
 
+    small[0].wait()
     x = h_ref[...].astype(F32)
     ss_send[...] = column_to_row(jnp.sum(x * x, axis=-1, keepdims=True))
     wait_barrier()
     ss = [remote(ss_send, ss_recv.at[i], ss_s.at[i], ss_r.at[i], 'dm', peer) for i, peer in enumerate((nxt, prv, far))]
     for copy in ss:
         copy.start()
+    for load in small[1:]:
+        load.wait()
     hd = cos_ref.shape[1]
     cos2[:, :hd] = cos_ref[...]
     cos2[:, hd:] = cos_ref[...]
@@ -73,7 +79,7 @@
         copy.wait_recv()
     total = ss_send[...] + ss_recv[0] + ss_recv[1] + ss_recv[2]
     scale = row_to_column(lax.rsqrt(total / width_full + EPS))
-    x_buf[...] = scale_rows(h_ref[...].astype(F32), scale, g_ref[...].astype(F32))
+    x_buf[...] = scale_rows(h_ref[...].astype(F32), scale, g_ref[...].astype(F32)[None, :])
 
     def block(owner, second):
         return pl.ds(pl.multiple_of(owner * rows + second * half, half), half)
@@ -124,14 +130,15 @@
     return pl.pallas_call(
         functools.partial(qkv_kernel, nd, width * nd),
         out_shape=[jax.ShapeDtypeStruct((rows, cols), F32)] * 3,
-        in_specs=[vmem] * 4 + [hbm] * 3,
+        in_specs=[hbm] * 7,
         out_specs=[vmem] * 3,
         scratch_shapes=[
+            pltpu.VMEM(hidden.shape, BF16), pltpu.VMEM(g.shape, BF16), pltpu.VMEM(cos.shape, F32), pltpu.VMEM(sin.shape, F32),
             pltpu.VMEM((3, heads, width, head), BF16), pltpu.VMEM((batch, width), BF16), pltpu.VMEM((3, batch, cols), F32),
             pltpu.VMEM((8, batch), F32), pltpu.VMEM((3, 8, batch), F32), piece, piece, piece, piece,
             pltpu.VMEM((rows, head), F32), pltpu.VMEM((rows, head), F32),
-            dma((3,)), dma((3,)), dma((3,))] + [dma((2, 3))] * 6,
-        compiler_params=pltpu.CompilerParams(collective_id=0, has_side_effects=True, vmem_limit_bytes=40 * 2 ** 20),
+            dma((4,)), dma((3,)), dma((3,)), dma((3,))] + [dma((2, 3))] * 6,
+        compiler_params=pltpu.CompilerParams(collective_id=0, has_side_effects=True, vmem_limit_bytes=VMEM_LIMIT),
         name='qkv',
     )(hidden, g, cos, sin, wq, wk, wv)
 
@@ -139,33 +146,39 @@
 def attend_kernel(lens_ref, q_ref, kn_ref, vn_ref, kc_ref, vc_ref, ko_ref, vo_ref, o_ref):
     step = pl.program_id(0)
     rb, heads, slots, head = kc_ref.shape
-    pos = lax.broadcasted_iota(jnp.int32, (heads, slots, head), 1)
-    head_row = lax.broadcasted_iota(jnp.int32, (8, heads * slots), 0)
-    lane = lax.broadcasted_iota(jnp.int32, (8, heads * slots), 1)
+    window = 16
+    span = heads * slots
+    pos = lax.broadcasted_iota(jnp.int32, (heads, window, head), 1)
+    head_row = lax.broadcasted_iota(jnp.int32, (8, span), 0)
+    lane = lax.broadcasted_iota(jnp.int32, (8, span), 1)
     lane_slot = lane % slots
     own_head = (lane // slots) == head_row
     q_row = lax.broadcasted_iota(jnp.int32, (8, head), 0)
-    q_all, kn_all, vn_all = q_ref[...], kn_ref[...], vn_ref[...]
+    q_all = q_ref[...]
+    ko_ref[...] = kc_ref[...]
+    vo_ref[...] = vc_ref[...]
+    lengths = [lens_ref[step * rb + r] for r in range(rb)]
     for r in range(rb):
-        length = lens_ref[step * rb + r]
-        write = pos == length
-
-        def new(vals):
-            return jnp.stack([jnp.broadcast_to(vals[r:r + 1, i * head:(i + 1) * head], (slots, head)) for i in range(heads)])
-
-        k = jnp.where(write, new(kn_all), kc_ref[r].astype(F32)).astype(BF16)
-        v = jnp.where(write, new(vn_all), vc_ref[r].astype(F32)).astype(BF16)
-        ko_ref[r] = k
-        vo_ref[r] = v
+        base = pl.multiple_of(lengths[r] // window * window, window)
+        write = pos == lengths[r] - base
+        for new_ref, old, out in ((kn_ref, kc_ref, ko_ref), (vn_ref, vc_ref, vo_ref)):
+            new = jnp.stack([jnp.broadcast_to(new_ref[r:r + 1, i * head:(i + 1) * head], (window, head)) for i in range(heads)])
+            out[r, :, pl.ds(base, window), :] = jnp.where(write, new, old[r, :, pl.ds(base, window), :].astype(F32)).astype(BF16)
+    scores, masks = [], []
+    for r in range(rb):
         q = jnp.zeros((8, head), F32)
         for i in range(heads):
             q = jnp.where(q_row == i, jnp.broadcast_to(q_all[r:r + 1, i * head:(i + 1) * head], (8, head)), q)
-        s = lax.dot_general(q.astype(BF16), k.reshape(heads * slots, head), (((1,), (1,)), ((), ())), preferred_element_type=F32)
-        s = jnp.where(own_head & (lane_slot <= length), s * (head ** -0.5), float(jnp.finfo(F32).min))
-        p = jnp.exp(s - jnp.max(s, axis=-1, keepdims=True))
-        p = jnp.where(own_head & (lane_slot <= length), p, 0.0)
-        p = (p / jnp.maximum(jnp.sum(p, axis=-1, keepdims=True), 1e-30)).astype(BF16)
-        o = jnp.dot(p, v.reshape(heads * slots, head), preferred_element_type=F32)
+        k = ko_ref[r].reshape(span, head)
+        s = lax.dot_general(q.astype(BF16), k, (((1,), (1,)), ((), ())), preferred_element_type=F32)
+        masks.append(own_head & (lane_slot <= lengths[r]))
+        scores.append(jnp.where(masks[r], s * (head ** -0.5), float(jnp.finfo(F32).min)))
+    s = jnp.stack(scores)
+    p = jnp.exp(s - jnp.max(s, axis=-1, keepdims=True))
+    p = jnp.where(jnp.stack(masks), p, 0.0)
+    p = (p / jnp.maximum(jnp.sum(p, axis=-1, keepdims=True), 1e-30)).astype(BF16)
+    for r in range(rb):
+        o = jnp.dot(p[r], vo_ref[r].reshape(span, head), preferred_element_type=F32)
         for i in range(heads):
             o_ref[r:r + 1, i * head:(i + 1) * head] = o[i:i + 1]
 
@@ -183,13 +196,14 @@
             out_specs=[cache_block, cache_block, row_block]),
         out_shape=[jax.ShapeDtypeStruct(kc.shape, BF16), jax.ShapeDtypeStruct(vc.shape, BF16),
                    jax.ShapeDtypeStruct((rows, heads * head), F32)],
-        compiler_params=pltpu.CompilerParams(vmem_limit_bytes=40 * 2 ** 20),
+        compiler_params=pltpu.CompilerParams(vmem_limit_bytes=VMEM_LIMIT),
+        cost_estimate=pl.CostEstimate(flops=4 * rows * heads * slots * head, bytes_accessed=4 * kc.size * 2, transcendentals=0),
         name='attend',
     )(lens, q, kn, vn, kc, vc)
 
 
-def mlp_kernel(nd, nx, width_full, o_ref, h_ref, g_ref, wo_hbm, wg_hbm, wu_hbm, wd_hbm, out_ref,
-               wo, wg, wu, wd, o_all, part, d2d_recv, xa_recv, xb_recv, xc_send, xc_recv, h1_buf, ss_send, ss_recv,
+def mlp_kernel(nd, nx, width_full, o_ref, h_hbm, g_hbm, wo_hbm, wg_hbm, wu_hbm, wd_hbm, out_ref,
+               h_ref, g_ref, wo, wg, wu, wd, o_all, part, d2d_recv, xa_recv, xb_recv, xc_send, xc_recv, h1_buf, ss_send, ss_recv,
                x2_all, gu, ga_recv, gb_recv, gc_send, gc_recv, m_all, h_all,
                w_sem, o_s, o_r, d_s, d_r, xa_s, xa_r, xb_s, xb_r, xc_s, xc_r, ss_s, ss_r,
                ag_s, ag_r, agf_s, agf_r, agd_s, agd_r, ga_s, ga_r, gb_s, gb_r, gc_s, gc_r, m_s, m_r, mf_s, mf_r):
@@ -218,7 +232,7 @@
 
     wait_barrier = entry_barrier([('dm', nxt), ('dm', prv), ('dm', far), ('tp', partner), ('tp', xpeer_ids[0]), ('tp', xpeer_ids[1])])
     loads = [pltpu.make_async_copy(src, dst, w_sem.at[i])
-             for i, (src, dst) in enumerate(((wo_hbm, wo), (wg_hbm, wg), (wu_hbm, wu), (wd_hbm, wd)))]
+             for i, (src, dst) in enumerate(((wo_hbm, wo), (wg_hbm, wg), (wu_hbm, wu), (wd_hbm, wd), (h_hbm, h_ref), (g_hbm, g_ref)))]
     for load in loads:
         load.start()
 
@@ -288,6 +302,8 @@
     for n in range(0, width, step):
         part[0, :, n:n + step] = jnp.dot(o_all[...], wo[:, n:n + step], preferred_element_type=F32)
     attn = tp_scatter(0)
+    loads[4].wait()
+    loads[5].wait()
     h1 = (h_ref[tile_rows(xi, core)] + attn.astype(BF16))
     h1_buf[...] = h1
     h1 = h1.astype(F32)
@@ -299,7 +315,7 @@
         got(ss_recv.at[i], ss_s.at[i], ss_r.at[i], 'dm', peer)
     total = ss_send[...] + ss_recv[0] + ss_recv[1] + ss_recv[2]
     scale = row_to_column(lax.rsqrt(total / width_full + EPS))[:share]
-    x2_all[tile_rows(xi, core)] = scale_rows(h1, scale, g_ref[...].astype(F32))
+    x2_all[tile_rows(xi, core)] = scale_rows(h1, scale, g_ref[...].astype(F32)[None, :])
     tp_gather(0, x2_all)
 
     loads[1].wait()
@@ -379,17 +395,18 @@
     return pl.pallas_call(
         functools.partial(mlp_kernel, nd, nx, width * nd),
         out_shape=jax.ShapeDtypeStruct((batch, width), BF16),
-        in_specs=[vmem] * 3 + [hbm] * 4,
+        in_specs=[vmem] + [hbm] * 6,
         out_specs=vmem,
         scratch_shapes=[
+            pltpu.VMEM(hidden.shape, BF16), pltpu.VMEM(g.shape, BF16),
             pltpu.VMEM(wo.shape, BF16), pltpu.VMEM(wg.shape, BF16), pltpu.VMEM(wu.shape, BF16), pltpu.VMEM(wd.shape, BF16),
             pltpu.VMEM((batch, inner), BF16), pltpu.VMEM((2, batch, width), F32), pltpu.VMEM((2, nx, share, width), F32),
             xpiece, xpiece, xpiece, xpiece, pltpu.VMEM((share, width), BF16), pltpu.VMEM((8, 128), F32), pltpu.VMEM((3, 8, 128), F32),
             pltpu.VMEM((batch, width), BF16), pltpu.VMEM((4, PARTS, 2, 2, ph, batch), F32), gpiece, gpiece, gpiece, gpiece,
             pltpu.VMEM((cols, batch), BF16), pltpu.VMEM((batch, width), BF16),
-            dma((4,)), dma((2, 2)), dma((2, 2)), dma((2, 4)), dma((2, 4))] + [dma((2, 2))] * 6 + [dma((3,))] * 2
+            dma((6,)), dma((2, 2)), dma((2, 2)), dma((2, 4)), dma((2, 4))] + [dma((2, 2))] * 6 + [dma((3,))] * 2
         + [dma((2, 2))] * 4 + [dma((2, 4))] * 2 + [dma((2, PARTS))] * 10,
-        compiler_params=pltpu.CompilerParams(collective_id=1, has_side_effects=True, vmem_limit_bytes=56 * 2 ** 20),
+        compiler_params=pltpu.CompilerParams(collective_id=1, has_side_effects=True, vmem_limit_bytes=VMEM_LIMIT),
         name='mlp',
     )(o, hidden, g, wo, wg, wu, wd)
 
@@ -405,9 +422,9 @@
 
     def local_layer(hidden, w_q, w_k, w_v, w_o, w_gate, w_up, w_down, norm_attn, norm_mlp, k_cache, v_cache, seq_lens, rope_cos, rope_sin):
         wq, wk, wv = (w.transpose(1, 0, 2) for w in (w_q, w_k, w_v))
-        q, kn, vn = qkv(nd, hidden, norm_attn[None, :], rope_cos, rope_sin, wq, wk, wv)
+        q, kn, vn = qkv(nd, hidden, norm_attn, rope_cos, rope_sin, wq, wk, wv)
         ko, vo, o = attend(seq_lens, q, kn, vn, k_cache.transpose(0, 2, 1, 3), v_cache.transpose(0, 2, 1, 3))
-        h_out = mlp(nd, nx, o, hidden, norm_mlp[None, :], w_o.reshape(-1, w_o.shape[-1]), w_gate.T, w_up.T, w_down)
+        h_out = mlp(nd, nx, o, hidden, norm_mlp, w_o.reshape(-1, w_o.shape[-1]), w_gate.T, w_up.T, w_down)
         return h_out, ko.transpose(0, 2, 1, 3), vo.transpose(0, 2, 1, 3)
 
     return jax.shard_map(local_layer, mesh=mesh, in_specs=in_specs, out_specs=out_specs, check_vma=False)

time: 160 us -> 137 us (0.86)
  local copies, waits for them, and re-layouts: 14.3 us -> 1.97 us
  Pallas kernels: 144 us -> 134 us
    pallas_call x1, Pallas kernels: 23 us -> 11.9 us  [attend(): pl.pallas_call(attend_kernel, grid_spec=pltpu.PrefetchScalarGridSpec(num_...]
    unnamed x21 -> x1, local copies, waits for them, and re-layouts: 12 us -> 1.97 us
    broadcast_in_dim x2 -> x0, local copies, waits for them, and re-layouts: 2.29 us -> none  [the longest x1 1.44 us: local_layer(): norm_mlp[None, :]]
where the time goes in v2:
time: 137 us
  Pallas kernels  134 us (98%)
  local copies, waits for them, and re-layouts  1.97 us (1%)
    pallas_call x1, Pallas kernels, mlp(): pl.pallas_call(functools.partial(mlp_kernel, nd, nx, width * nd), out_sha...  95.1 us
    pallas_call x1, Pallas kernels, qkv(): pl.pallas_call(functools.partial(qkv_kernel, nd, width * nd), out_shape=[...  26.9 us
    pallas_call x1, Pallas kernels, attend(): pl.pallas_call(attend_kernel, grid_spec=pltpu.PrefetchScalarGridSpec(num_...  11.9 us

profile of v2, /device:TPU:97, one launch (start us, length us, event | category | flops | bytes accessed | tf_op | source)
XLA Modules:
  0.0 136.5 jit_solution(7005526222839010907)
XLA Ops:
  0.6 26.9 %qkv.1 = (f32[64,640]{1,0:T(8,128)}, f32[64,640]{1,0:T(8,128)}, f32[64,640]{1,0:T(8,128)}) custom-call(bf16[256,1280]{1,0:T(8,128)(2,1)} %h_hbm.3, bf16[1280]{0:T(1024)(128)(2,1)} %g_hbm.2, f32[64,64]{1,0:T(8,128)} %cos_hbm.1, f32[64,64]{1,0:T(8,128)} %sin_hbm.1, bf16[5,1280,128]{2,1,0:T(8,128)(2,1)} %bitcast.15, bf16[5,1280,128]{2,1,0:T(8,128)(2,1)} %bitcast.16, ...), custom_call_target="tpu_custom_call" | custom-call | tf_op jit(solution)/shard_map/qkv/pallas_call | solution.py:130
  27.6 11.9 %attend.1 = (bf16[64,5,64,128]{3,2,1,0:T(8,128)(2,1)}, bf16[64,5,64,128]{3,2,1,0:T(8,128)(2,1)}, f32[64,640]{1,0:T(8,128)}) custom-call(s32[64]{0:T(128)} %lens_ref.1, f32[64,640]{1,0:T(8,128)} %get-tuple-element.9.q_ref, f32[64,640]{1,0:T(8,128)} %get-tuple-element.10.kn_ref, f32[64,640]{1,0:T(8,128)} %get-tuple-element.11.vn_ref, ...), custom_call_target="tpu_custom_call" | custom-call | flops 10485760 | bytes 20971520 | tf_op jit(solution)/shard_map/attend/pallas_call | solution.py:191
  39.5 95.1 %mlp.1 = bf16[256,1280]{1,0:T(8,128)(2,1)} custom-call(f32[64,640]{1,0:T(8,128)} %get-tuple-element.12.o_ref, bf16[256,1280]{1,0:T(8,128)(2,1)} %h_hbm.3, bf16[1280]{0:T(1024)(128)(2,1)} %g_hbm.3, bf16[640,1280]{1,0:T(8,128)(2,1)} %bitcast.14, bf16[1728,1280]{1,0:T(8,128)(2,1)} %bitcast.12, bf16[1728,1280]{1,0:T(8,128)(2,1)} %bitcast.13, ...), custom_call_target="tpu_custom_call" | custom-call | tf_op jit(solution)/shard_map/mlp/pallas_call | solution.py:395
  134.6 2.0 %copy.19 = bf16[256,1280]{1,0:T(8,128)(2,1)} copy(bf16[256,1280]{1,0:T(8,128)(2,1)} %mlp.1) | data formatting | bytes 1310720

commit v3 on v0

v3 whole, which is shorter than its diff:
```python
import functools

import jax
import jax.numpy as jnp
from jax import lax
from jax.experimental import pallas as pl
from jax.experimental.pallas import tpu as pltpu
from jax.sharding import PartitionSpec as P

EPS = 1e-6
F32 = jnp.float32
BF16 = jnp.bfloat16
MESH = pl.DeviceIdType.MESH
VMEM_LIMIT = 63 * 2 ** 20
BATCHES = 2
PARTS = 3


def remote(src, dst, send, recv, axis, index):
    return pltpu.make_async_remote_copy(
        src_ref=src, dst_ref=dst, send_sem=send, recv_sem=recv, device_id={axis: index}, device_id_type=MESH)


def entry_barrier(peers):
    barrier = pltpu.get_barrier_semaphore()
    for axis, index in peers:
        pl.semaphore_signal(barrier, inc=1, device_id={axis: index}, device_id_type=MESH)
    return lambda: pl.semaphore_wait(barrier, len(peers))


def column_to_row(col):
    rows = col.shape[0]
    return jnp.concatenate(
        [jnp.broadcast_to(col[i:i + 128], (128, 128)).T[:8] for i in range(0, rows, 128)], axis=1)


def row_to_column(row):
    rows = row.shape[1]
    return jnp.concatenate(
        [jnp.broadcast_to(row[:1, i:i + 128], (128, 128)).T for i in range(0, rows, 128)], axis=0)


def scale_rows(x, scale, gain):
    width = x.shape[1]
    cols = [x[:, i:i + 128] * scale * gain[:, i:i + 128] for i in range(0, width, 128)]
    return jnp.concatenate(cols, axis=1).astype(BF16)


def layer_kernel(nd, nx, width_full, lens_ref, h_hbm, g1_hbm, g2_hbm, cos_hbm, sin_hbm, wq_hbm, wk_hbm, wv_hbm, wo_hbm, wg_hbm, wu_hbm, wd_hbm,
                 kc_hbm, vc_hbm, out_ref, k_out, v_out,
                 h_ref, g1_ref, g2_ref, cos_ref, sin_ref, wqkv, wo, wg, wu, wd, kc, vc,
                 x_buf, part, ss_send, ss_recv, a_recv, b_recv, c_send, c_recv, cos2, sin2, q_buf, o_own,
                 o_all, full, d2d_recv, xa_recv, xb_recv, xc_send, xc_recv, h1_buf, st_send, st_recv, x2_all,
                 gu, ga_recv, gb_recv, gc_send, gc_recv, m_all, h_all,
                 w_sem, ss_s, ss_r, a_s, a_r, b_s, b_r, c_s, c_r, o_s, o_r, d_s, d_r, xa_s, xa_r, xb_s, xb_r, xc_s, xc_r,
                 st_s, st_r, ag_s, ag_r, agf_s, agf_r, agd_s, agd_r, ga_s, ga_r, gb_s, gb_r, gc_s, gc_r, m_s, m_r, mf_s, mf_r):
    dm, tp = lax.axis_index('dm'), lax.axis_index('tp')
    nxt, prv, far = lax.rem(dm + 1, nd), lax.rem(dm + nd - 1, nd), lax.rem(dm + 2, nd)
    core, xi = lax.rem(tp, 2), tp // 2
    xn, xp, xf = lax.rem(xi + 1, nx), lax.rem(xi + nx - 1, nx), lax.rem(xi + 2, nx)
    partner = tp + 1 - 2 * core
    ypeers, xpeers, xids = (nxt, prv), (xn, xp), (2 * xn + core, 2 * xp + core)
    batch, width = h_ref.shape
    heads, slots, head = kc.shape[1:]
    rows = batch // nd
    rb = rows // BATCHES
    rh = rb // 2
    brows = nd * rb
    share = brows // (2 * nx)
    sh = share // 2
    cols = wd.shape[0]
    own_cols = cols // nd
    pc = own_cols // PARTS
    ph = pc // 2
    sends = []

    def go(*args):
        sends.append(remote(*args))
        sends[-1].start()

    def got(ref, send, recv, axis, index):
        remote(ref, ref, send, recv, axis, index).wait_recv()

    def al(x, n):
        return pl.multiple_of(x, n)

    wait_barrier = entry_barrier([('dm', nxt), ('dm', prv), ('dm', far), ('tp', partner), ('tp', xids[0]), ('tp', xids[1])])
    pairs = ((h_hbm, h_ref), (wq_hbm, wqkv.at[0]), (wk_hbm, wqkv.at[1]), (wv_hbm, wqkv.at[2]), (g1_hbm, g1_ref), (cos_hbm, cos_ref), (sin_hbm, sin_ref),
             (kc_hbm, kc), (vc_hbm, vc), (wo_hbm, wo), (g2_hbm, g2_ref), (wg_hbm, wg), (wu_hbm, wu), (wd_hbm, wd))
    loads = [pltpu.make_async_copy(src, dst, w_sem.at[i]) for i, (src, dst) in enumerate(pairs)]
    for load in loads[:7]:
        load.start()
    loads[0].wait()
    x = h_ref[...].astype(F32)
    ss_send[...] = column_to_row(jnp.sum(x * x, axis=-1, keepdims=True))
    wait_barrier()
    for i, peer in enumerate((nxt, prv, far)):
        go(ss_send, ss_recv.at[i], ss_s.at[i], ss_r.at[i], 'dm', peer)
    for load in loads[4:7]:
        load.wait()
    hd = cos_ref.shape[1]
    cos2[:, :hd] = cos_ref[...]
    cos2[:, hd:] = cos_ref[...]
    sin2[:, :hd] = -sin_ref[...]
    sin2[:, hd:] = sin_ref[...]
    for i, peer in enumerate((nxt, prv, far)):
        got(ss_recv.at[i], ss_s.at[i], ss_r.at[i], 'dm', peer)
    for load in loads[1:4]:
        load.wait()
    for load in loads[7:]:
        load.start()
    total = ss_send[...] + ss_recv[0] + ss_recv[1] + ss_recv[2]
    scale = row_to_column(lax.rsqrt(total / width_full + EPS))
    x_buf[...] = scale_rows(h_ref[...].astype(F32), scale, g1_ref[...].astype(F32)[None, :])

    def prow(owner, b, s):
        return pl.ds(al(owner * rows + b * rb + s * rh, rh), rh)

    def qkv_a(b, t):
        for d in range(2):
            go(part.at[t, prow(far, b, d)], a_recv.at[b, d, t], a_s.at[b, d, t], a_r.at[b, d, t], 'dm', ypeers[d])

    def qkv_b(b, t):
        for d in range(2):
            go(part.at[t, prow(ypeers[d], b, 1 - d)], b_recv.at[b, d, t], b_s.at[b, d, t], b_r.at[b, d, t], 'dm', ypeers[d])

    def qkv_c(b, t):
        for d in range(2):
            got(a_recv.at[b, d, t], a_s.at[b, d, t], a_r.at[b, d, t], 'dm', ypeers[d])
            c_send[b, d, t] = a_recv[b, d, t] + part[t, prow(ypeers[d], b, d)]
            go(c_send.at[b, d, t], c_recv.at[b, d, t], c_s.at[b, d, t], c_r.at[b, d, t], 'dm', ypeers[d])

    def totals(b):
        for t, out in enumerate((q_buf, k_out, v_out)):
            for d in range(2):
                got(b_recv.at[b, d, t], b_s.at[b, d, t], b_r.at[b, d, t], 'dm', ypeers[d])
                got(c_recv.at[b, d, t], c_s.at[b, d, t], c_r.at[b, d, t], 'dm', ypeers[d])
            for d in range(2):
                tot = part[t, prow(dm, b, d)] + c_recv[b, d, t] + b_recv[b, 1 - d, t]
                here = slice(b * rb + d * rh, b * rb + (d + 1) * rh)
                for i in range(heads):
                    y = tot[:, i * head:(i + 1) * head]
                    if t < 2:
                        y = y * cos2[here] + pltpu.roll(y, head // 2, 1) * sin2[here]
                    out[here, i * head:(i + 1) * head] = y.astype(BF16).astype(F32)

    span = heads * slots
    group = 8

    def attention(lo, hi):
        lane = lax.broadcasted_iota(jnp.int32, (8, span), 1)
        lane_slot = lane % slots
        own_head = (lane // slots) == lax.broadcasted_iota(jnp.int32, (8, span), 0)
        head_row = lax.broadcasted_iota(jnp.int32, (8, head), 0)

        def body(g, carry):
            first = al(g * group, group)
            vals = [ref[pl.ds(first, group), :] for ref in (q_buf, k_out, v_out)]

            def per_head(val, r):
                y = jnp.zeros((8, head), F32)
                for i in range(heads):
                    y = jnp.where(head_row == i, jnp.broadcast_to(val[r:r + 1, i * head:(i + 1) * head], (8, head)), y)
                return y

            scores, masks, news = [], [], []
            for r in range(group):
                q = per_head(vals[0], r)
                k = kc[first + r].reshape(span, head)
                s = lax.dot_general(q.astype(BF16), k, (((1,), (1,)), ((), ())), preferred_element_type=F32)
                masks.append(own_head & (lane_slot < lens_ref[first + r]))
                scores.append(jnp.where(masks[r], s * (head ** -0.5), float(jnp.finfo(F32).min)))
                news.append(jnp.sum(q * per_head(vals[1], r), axis=-1, keepdims=True) * (head ** -0.5))
            s, new = jnp.stack(scores), jnp.stack(news)
            top = jnp.maximum(jnp.max(s, axis=-1, keepdims=True), new)
            p = jnp.where(jnp.stack(masks), jnp.exp(s - top), 0.0)
            p_new = jnp.exp(new - top)
            den = jnp.sum(p, axis=-1, keepdims=True) + p_new
            p = (p / den).astype(BF16)
            p_new = (p_new / den).astype(BF16).astype(F32)
            for r in range(group):
                o = jnp.dot(p[r], vc[first + r].reshape(span, head), preferred_element_type=F32) + p_new[r] * per_head(vals[2], r)
                for i in range(heads):
                    o_own[g, r:r + 1, i * head:(i + 1) * head] = o[i:i + 1]
            return carry

        lax.fori_loop(lo, hi, body, 0)

    def orow(owner, s=0, n=rb):
        return pl.ds(al(owner * rb + s, 16), n)

    def o_send(b):
        o_all[b, orow(dm)] = o_own[b * rb // group:(b + 1) * rb // group].reshape(rb, heads * head).astype(BF16)
        for d in range(2):
            mine = o_all.at[b, orow(dm)]
            go(mine, mine, o_s.at[0, b, d], o_r.at[0, b, d], 'dm', ypeers[d])

    def o_fwd(b):
        for d in range(2):
            got(o_all.at[b, orow(ypeers[1 - d])], o_s.at[0, b, d], o_r.at[0, b, d], 'dm', ypeers[d])
            piece = o_all.at[b, orow(ypeers[1 - d], d * rh, rh)]
            go(piece, piece, o_s.at[1, b, d], o_r.at[1, b, d], 'dm', ypeers[d])

    def o_done(b):
        for d in range(2):
            got(o_all.at[b, orow(far, d * rh, rh)], o_s.at[1, b, d], o_r.at[1, b, d], 'dm', ypeers[d])

    def trow(owner, c, s=0, n=share):
        return pl.ds(al(c * (brows // 2) + owner * share + s, sh), n)

    order = (xf, xn, xp, xi)

    def xs_pair(u, b):
        for i, owner in enumerate(order):
            go(full.at[u, b, trow(owner, 1 - core)], d2d_recv.at[u, b, i], d_s.at[u, b, i], d_r.at[u, b, i], 'tp', partner)

    def xs_ab(u, b):
        for i, owner in enumerate(order):
            got(d2d_recv.at[u, b, i], d_s.at[u, b, i], d_r.at[u, b, i], 'tp', partner)
            here = trow(owner, core)
            full[u, b, here] = full[u, b, here] + d2d_recv[u, b, i]
            if i == 0:
                for d in range(2):
                    go(full.at[u, b, trow(xf, core, d * sh, sh)], xa_recv.at[u, b, d], xa_s.at[u, b, d], xa_r.at[u, b, d], 'tp', xids[d])
            elif i < 3:
                d = i - 1
                go(full.at[u, b, trow(owner, core, (1 - d) * sh, sh)], xb_recv.at[u, b, d], xb_s.at[u, b, d], xb_r.at[u, b, d], 'tp', xids[d])

    def xs_c(u, b):
        for d in range(2):
            got(xa_recv.at[u, b, d], xa_s.at[u, b, d], xa_r.at[u, b, d], 'tp', xids[d])
            xc_send[u, b, d] = xa_recv[u, b, d] + full[u, b, trow(xpeers[d], core, d * sh, sh)]
            go(xc_send.at[u, b, d], xc_recv.at[u, b, d], xc_s.at[u, b, d], xc_r.at[u, b, d], 'tp', xids[d])

    def xs_done(u, b):
        for d in range(2):
            got(xb_recv.at[u, b, d], xb_s.at[u, b, d], xb_r.at[u, b, d], 'tp', xids[d])
            got(xc_recv.at[u, b, d], xc_s.at[u, b, d], xc_r.at[u, b, d], 'tp', xids[d])
        return jnp.concatenate(
            [full[u, b, trow(xi, core, d * sh, sh)] + xc_recv[u, b, d] + xb_recv[u, b, 1 - d] for d in range(2)], axis=0)

    def lanes(d):
        return pl.ds(d * (width // 2), width // 2)

    def ag_send(u, buf, b):
        mine = buf.at[b, trow(xi, core)]
        for d in range(2):
            go(mine, mine, ag_s.at[u, b, d], ag_r.at[u, b, d], 'tp', xids[d])
        go(mine, mine, agd_s.at[u, b, 0], agd_r.at[u, b, 0], 'tp', partner)

    def ag_fwd(u, buf, b):
        for d in range(2):
            near = buf.at[b, trow(xpeers[1 - d], core)]
            got(near, ag_s.at[u, b, d], ag_r.at[u, b, d], 'tp', xids[d])
            piece = buf.at[b, trow(xpeers[1 - d], core), lanes(d)]
            go(piece, piece, agf_s.at[u, b, d], agf_r.at[u, b, d], 'tp', xids[d])
            go(near, near, agd_s.at[u, b, 1 + d], agd_r.at[u, b, 1 + d], 'tp', partner)

    def ag_done(u, buf, b):
        for d in range(2):
            got(buf.at[b, trow(xf, core), lanes(d)], agf_s.at[u, b, d], agf_r.at[u, b, d], 'tp', xids[d])
        last = buf.at[b, trow(xf, core)]
        go(last, last, agd_s.at[u, b, 3], agd_r.at[u, b, 3], 'tp', partner)
        for i, owner in enumerate((xi, xp, xn, xf)):
            got(buf.at[b, trow(owner, 1 - core)], agd_s.at[u, b, i], agd_r.at[u, b, i], 'tp', partner)

    step = 256

    def o_proj(b):
        for n in range(0, width, step):
            full[0, b, :, n:n + step] = jnp.dot(o_all[b], wo[:, n:n + step], preferred_element_type=F32)
        xs_pair(0, b)

    def norm_send(b):
        attn = xs_done(0, b)
        first = trow(xi, core).start
        owner = first // rb
        here = pl.ds(al(owner * rows + b * rb + (first - owner * rb), share), share)
        h1 = h_ref[here] + attn.astype(BF16)
        h1_buf[b] = h1
        h1 = h1.astype(F32)
        col = jnp.sum(h1 * h1, axis=-1, keepdims=True)
        st_send[b] = column_to_row(jnp.concatenate([col] * (128 // share), axis=0))
        for i, peer in enumerate((nxt, prv, far)):
            go(st_send.at[b], st_recv.at[b, i], st_s.at[b, i], st_r.at[b, i], 'dm', peer)

    def norm_done(b):
        for i, peer in enumerate((nxt, prv, far)):
            got(st_recv.at[b, i], st_s.at[b, i], st_r.at[b, i], 'dm', peer)
        total = st_send[b] + st_recv[b, 0] + st_recv[b, 1] + st_recv[b, 2]
        scale = row_to_column(lax.rsqrt(total / width_full + EPS))[:share]
        x2_all[b, trow(xi, core)] = scale_rows(h1_buf[b].astype(F32), scale, g2_ref[...].astype(F32)[None, :])
        ag_send(0, x2_all, b)

    def columns(owner):
        return pl.ds(al(owner * own_cols, 16), own_cols)

    def gu_ab(b):
        for i, owner in enumerate((far, nxt, prv, dm)):
            for j, w in enumerate((wg, wu)):
                y = lax.dot_general(w[columns(owner)], x2_all[b], (((1,), (1,)), ((), ())), preferred_element_type=F32)
                for p in range(PARTS):
                    for s in range(2):
                        gu[b, i, p, s, j] = y[p * pc + s * ph:p * pc + (s + 1) * ph]
            for p in range(PARTS):
                if i == 0:
                    for d in range(2):
                        go(gu.at[b, 0, p, d], ga_recv.at[b, d, p], ga_s.at[b, d, p], ga_r.at[b, d, p], 'dm', ypeers[d])
                elif i < 3:
                    d = i - 1
                    go(gu.at[b, i, p, 1 - d], gb_recv.at[b, d, p], gb_s.at[b, d, p], gb_r.at[b, d, p], 'dm', ypeers[d])

    def gu_c(b):
        for p in range(PARTS):
            for d in range(2):
                got(ga_recv.at[b, d, p], ga_s.at[b, d, p], ga_r.at[b, d, p], 'dm', ypeers[d])
                gc_send[b, d, p] = ga_recv[b, d, p] + gu[b, 1 + d, p, d]
                go(gc_send.at[b, d, p], gc_recv.at[b, d, p], gc_s.at[b, d, p], gc_r.at[b, d, p], 'dm', ypeers[d])

    cut = (pc // 2 + 15) // 16 * 16
    cuts = ((0, cut), (cut, pc - cut))

    def mrow(owner, p, s=0, n=pc):
        return pl.ds(al(owner * own_cols + p * pc + s, 16), n)

    def m_send(b):
        for p in range(PARTS):
            for d in range(2):
                got(gb_recv.at[b, d, p], gb_s.at[b, d, p], gb_r.at[b, d, p], 'dm', ypeers[d])
                got(gc_recv.at[b, d, p], gc_s.at[b, d, p], gc_r.at[b, d, p], 'dm', ypeers[d])
            halves = []
            for d in range(2):
                gate, up = (gu[b, 3, p, d, j] + gc_recv[b, d, p, j] + gb_recv[b, 1 - d, p, j] for j in range(2))
                halves.append(gate * jax.nn.sigmoid(gate) * up)
            m_all[b, mrow(dm, p)] = jnp.concatenate(halves, axis=0).astype(BF16)
            for d in range(2):
                mine = m_all.at[b, mrow(dm, p)]
                go(mine, mine, m_s.at[b, d, p], m_r.at[b, d, p], 'dm', ypeers[d])

    def m_fwd(b):
        for p in range(PARTS):
            for d in range(2):
                got(m_all.at[b, mrow(ypeers[1 - d], p)], m_s.at[b, d, p], m_r.at[b, d, p], 'dm', ypeers[d])
                piece = m_all.at[b, mrow(ypeers[1 - d], p, *cuts[d])]
                go(piece, piece, mf_s.at[b, d, p], mf_r.at[b, d, p], 'dm', ypeers[d])

    def m_done(b):
        for p in range(PARTS):
            for d in range(2):
                got(m_all.at[b, mrow(far, p, *cuts[d])], mf_s.at[b, d, p], mf_r.at[b, d, p], 'dm', ypeers[d])

    def down(b):
        for n in range(0, width, step):
            full[1, b, :, n:n + step] = lax.dot_general(m_all[b], wd[:, n:n + step], (((0,), (0,)), ((), ())), preferred_element_type=F32)
        xs_pair(1, b)

    def h_send(b):
        mlp = xs_done(1, b)
        h_all[b, trow(xi, core)] = h1_buf[b] + mlp.astype(BF16)
        ag_send(1, h_all, b)

    def h_done(b):
        ag_done(1, h_all, b)
        for owner in range(nd):
            out_ref[owner * rows + b * rb:owner * rows + (b + 1) * rb] = h_all[b, owner * rb:(owner + 1) * rb]

    for t in range(3):
        for i in range(heads):
            part[t, :, i * head:(i + 1) * head] = jnp.dot(x_buf[...], wqkv[t, i], preferred_element_type=F32)
        qkv_a(0, t)
        qkv_b(0, t)
    qkv_a(1, 0)
    for t in range(3):
        qkv_c(0, t)
    qkv_a(1, 1)
    qkv_a(1, 2)
    for t in range(3):
        qkv_b(1, t)
    qkv_c(1, 0)
    totals(0)
    loads[7].wait()
    loads[8].wait()
    groups = rb // group
    attention(0, groups)
    o_send(0)
    qkv_c(1, 1)
    qkv_c(1, 2)
    o_fwd(0)
    totals(1)
    o_done(0)
    loads[9].wait()
    o_proj(0)
    attention(groups, groups + groups // 2)
    xs_ab(0, 0)
    attention(groups + groups // 2, 2 * groups)
    o_send(1)
    xs_c(0, 0)
    o_fwd(1)
    loads[10].wait()
    norm_send(0)
    o_done(1)
    o_proj(1)
    norm_done(0)
    xs_ab(0, 1)
    ag_fwd(0, x2_all, 0)
    xs_c(0, 1)
    for load in loads[11:]:
        load.wait()
    ag_done(0, x2_all, 0)
    gu_ab(0)
    norm_send(1)
    gu_c(0)
    norm_done(1)
    ag_fwd(0, x2_all, 1)
    ag_done(0, x2_all, 1)
    gu_ab(1)
    m_send(0)
    gu_c(1)
    m_fwd(0)
    m_done(0)
    down(0)
    xs_ab(1, 0)
    m_send(1)
    xs_c(1, 0)
    m_fwd(1)
    h_send(0)
    m_done(1)
    down(1)
    ag_fwd(1, h_all, 0)
    xs_ab(1, 1)
    xs_c(1, 1)
    h_done(0)
    h_send(1)
    ag_fwd(1, h_all, 1)
    h_done(1)
    for copy in sends:
        copy.wait_send()


def layer(nd, nx, lens, hidden, g1, g2, cos, sin, wq, wk, wv, wo, wg, wu, wd, kc, vc):
    batch, width = hidden.shape
    heads, _, head = wq.shape
    rows, inner, cols = batch // nd, heads * head, wd.shape[0]
    nb = BATCHES
    rh = rows // nb // 2
    brows = batch // nb
    share = brows // (2 * nx)
    vmem = pl.BlockSpec(memory_space=pltpu.VMEM)
    hbm = pl.BlockSpec(memory_space=pl.ANY)
    smem = pl.BlockSpec(memory_space=pltpu.SMEM)
    vm = pltpu.VMEM
    dma = pltpu.SemaphoreType.DMA
    piece = vm((nb, 2, 3, rh, inner), F32)
    xpiece = vm((2, nb, 2, share // 2, width), F32)
    ph = cols // nd // PARTS // 2
    gpiece = vm((nb, 2, PARTS, 2, ph, brows), F32)
    return pl.pallas_call(
        functools.partial(layer_kernel, nd, nx, width * nd),
        out_shape=[jax.ShapeDtypeStruct((batch, width), BF16), jax.ShapeDtypeStruct((rows, inner), F32), jax.ShapeDtypeStruct((rows, inner), F32)],
        in_specs=[smem] + [hbm] * 14,
        out_specs=[vmem] * 3,
        scratch_shapes=[
            vm(hidden.shape, BF16), vm(g1.shape, BF16), vm(g2.shape, BF16), vm(cos.shape, F32), vm(sin.shape, F32),
            vm((3, heads, width, head), BF16), vm(wo.shape, BF16), vm(wg.shape, BF16), vm(wu.shape, BF16), vm(wd.shape, BF16),
            vm(kc.shape, BF16), vm(vc.shape, BF16),
            vm((batch, width), BF16), vm((3, batch, inner), F32), vm((8, batch), F32), vm((3, 8, batch), F32),
            piece, piece, piece, piece, vm((rows, head), F32), vm((rows, head), F32), vm((rows, inner), F32), vm((rows // 8, 8, inner), F32),
            vm((nb, brows, inner), BF16), vm((2, nb, brows, width), F32), vm((2, nb, nx, share, width), F32),
            xpiece, xpiece, xpiece, xpiece, vm((nb, share, width), BF16), vm((nb, 8, 128), F32), vm((nb, 3, 8, 128), F32), vm((nb, brows, width), BF16),
            vm((nb, 4, PARTS, 2, 2, ph, brows), F32), gpiece, gpiece, gpiece, gpiece, vm((nb, cols, brows), BF16), vm((nb, brows, width), BF16),
            dma((14,)), dma((3,)), dma((3,))] + [dma((nb, 2, 3))] * 6 + [dma((2, nb, 2))] * 2 + [dma((2, nb, nx))] * 2 + [dma((2, nb, 2))] * 6
        + [dma((nb, 3))] * 2 + [dma((2, nb, 2))] * 4 + [dma((2, nb, nx))] * 2 + [dma((nb, 2, PARTS))] * 10,
        compiler_params=pltpu.CompilerParams(collective_id=0, has_side_effects=True, vmem_limit_bytes=VMEM_LIMIT),
        name='layer',
    )(lens, hidden, g1, g2, cos, sin, wq, wk, wv, wo, wg, wu, wd, kc, vc)


def update_kernel(lens_ref, kn_ref, vn_ref, h_ref, kc_ref, vc_ref, ko_ref, vo_ref, out_ref):
    step = pl.program_id(0)
    rb, heads, slots, head = kc_ref.shape
    window = 16
    pos = lax.broadcasted_iota(jnp.int32, (heads, window, head), 1)
    out_ref[...] = h_ref[...]
    ko_ref[...] = kc_ref[...]
    vo_ref[...] = vc_ref[...]
    for r in range(rb):
        length = lens_ref[step * rb + r]
        base = pl.multiple_of(length // window * window, window)
        write = pos == length - base
        for new_ref, old, out in ((kn_ref, kc_ref, ko_ref), (vn_ref, vc_ref, vo_ref)):
            new = jnp.stack([jnp.broadcast_to(new_ref[r:r + 1, i * head:(i + 1) * head], (window, head)) for i in range(heads)])
            out[r, :, pl.ds(base, window), :] = jnp.where(write, new, old[r, :, pl.ds(base, window), :].astype(F32)).astype(BF16)


def update(lens, kn, vn, h, kc, vc):
    rows, heads, slots, head = kc.shape
    rb = 8
    steps = rows // rb
    row_block = pl.BlockSpec((rb, heads * head), lambda i, lens: (i, 0))
    h_block = pl.BlockSpec((h.shape[0] // steps, h.shape[1]), lambda i, lens: (i, 0))
    cache_block = pl.BlockSpec((rb, heads, slots, head), lambda i, lens: (i, 0, 0, 0))
    return pl.pallas_call(
        update_kernel,
        grid_spec=pltpu.PrefetchScalarGridSpec(
            num_scalar_prefetch=1, grid=(steps,),
            in_specs=[row_block] * 2 + [h_block] + [cache_block] * 2,
            out_specs=[cache_block, cache_block, h_block]),
        out_shape=[jax.ShapeDtypeStruct(kc.shape, BF16), jax.ShapeDtypeStruct(vc.shape, BF16), jax.ShapeDtypeStruct(h.shape, BF16)],
        compiler_params=pltpu.CompilerParams(vmem_limit_bytes=VMEM_LIMIT),
        name='update',
    )(lens, kn, vn, h, kc, vc)


def solution(mesh):
    nd, nx = mesh.shape['dm'], mesh.shape['tp'] // 2
    row_spec = P('dp', 'dm')
    cache_spec = P(('dp', 'dm'), None, 'tp', None)
    batch_spec = P(('dp', 'dm'))
    rope_spec = P(('dp', 'dm'), None)
    in_specs = (row_spec, P('dm', 'tp', None), P('dm', 'tp', None), P('dm', 'tp', None), P('tp', None, 'dm'), P('dm', 'tp'), P('dm', 'tp'), P('tp', 'dm'), P('dm'), P('dm'), cache_spec, cache_spec, batch_spec, rope_spec, rope_spec)
    out_specs = (row_spec, cache_spec, cache_spec)

    def local_layer(hidden, w_q, w_k, w_v, w_o, w_gate, w_up, w_down, norm_attn, norm_mlp, k_cache, v_cache, seq_lens, rope_cos, rope_sin):
        wq, wk, wv = (w.transpose(1, 0, 2) for w in (w_q, w_k, w_v))
        kc, vc = (c.transpose(0, 2, 1, 3) for c in (k_cache, v_cache))
        h_out, kn, vn = layer(nd, nx, seq_lens, hidden, norm_attn, norm_mlp, rope_cos, rope_sin, wq, wk, wv, w_o.reshape(-1, w_o.shape[-1]), w_gate.T, w_up.T, w_down, kc, vc)
        ko, vo, h_out = update(seq_lens, kn, vn, h_out, kc, vc)
        return h_out, ko.transpose(0, 2, 1, 3), vo.transpose(0, 2, 1, 3)

    return jax.shard_map(local_layer, mesh=mesh, in_specs=in_specs, out_specs=out_specs, check_vma=False)
```

time: 330 us -> 141 us (0.43)
  Pallas kernels: 0 us -> 140 us
  blocking collectives: 134 us -> 0 us
  waiting for transfers between devices: 132 us -> 0 us
  matrix products: 32.4 us -> 0 us
  other arithmetic: 14.9 us -> 0 us
  between operations: 13.9 us -> 0.64 us
    pallas_call x0 -> x2, Pallas kernels: none -> 140 us  [the longest x1 129 us: layer(): pl.pallas_call(functools.partial(layer_kernel, nd, nx, width * nd), out_s...]
    psum x4 -> x0, blocking collectives: 124 us -> none  [the longest x1 54.9 us: local_layer(): attn_out = lax.psum(attn_part, 'tp').astype(jnp.bfloat16)]
    psum x1 -> x0, waiting for transfers between devices: 76.9 us -> none  [local_layer(): lax.psum(jnp.dot(x_mlp, w_up, preferred_element_type=jnp.float32), 'dm')]
    reduce_scatter x3 -> x0, waiting for transfers between devices: 55.4 us -> none  [the longest x1 22.2 us: local_layer(): q_rows = lax.psum_scatter(q_part, 'dm', scatter_dimension=0, tiled=True)]
    dot_general x9 -> x0, matrix products: 32.4 us -> none  [the longest x1 5.84 us: local_layer(): jnp.dot(gated_act, w_down, preferred_element_type=jnp.float32)]
    all_gather x1 -> x0, blocking collectives: 10.6 us -> none  [local_layer(): heads_all = lax.all_gather(attn_heads, 'dm', axis=0, tiled=True)]
    select_n x1 -> x0, other arithmetic: 7.41 us -> none  [attend(): k_out = jnp.where(write_mask, k_rot[:, None], k_cache)]
  transfers between devices with their start and end apart: 4 -> 0, of which waited for: 4 -> 0; matrix products, arithmetic and copies ran while one was open for 2% -> 0% of each run, Pallas kernels for 0% -> 0%
where the time goes in v3:
time: 141 us
  Pallas kernels  140 us (99%)
    pallas_call x1, Pallas kernels, layer(): pl.pallas_call(functools.partial(layer_kernel, nd, nx, width * nd), out_s...  129 us
    pallas_call x1, Pallas kernels, update(): pl.pallas_call(update_kernel, grid_spec=pltpu.PrefetchScalarGridSpec(num_...  11.4 us

profile of v3, /device:TPU:97, one launch (start us, length us, event | category | flops | bytes accessed | tf_op | source)
XLA Modules:
  0.0 141.1 jit_solution(14442936668552903277)
XLA Ops:
  0.6 129.0 %layer.1 = (bf16[256,1280]{1,0:T(8,128)(2,1)}, f32[64,640]{1,0:T(8,128)}, f32[64,640]{1,0:T(8,128)}) custom-call(s32[64]{0:T(128)} %lens_ref.3, bf16[256,1280]{1,0:T(8,128)(2,1)} %h_hbm.1, bf16[1280]{0:T(1024)(128)(2,1)} %g1_hbm.1, bf16[1280]{0:T(1024)(128)(2,1)} %g2_hbm.1, f32[64,64]{1,0:T(8,128)} %cos_hbm.1, f32[64,64]{1,0:T(8,128)} %sin_hbm.1, ...), custom_call_target="tpu_custom_call" | custom-call | tf_op jit(solution)/shard_map/layer/pallas_call | solution.py:457
  129.7 11.4 %update.1 = (bf16[64,5,64,128]{3,2,1,0:T(8,128)(2,1)}, bf16[64,5,64,128]{3,2,1,0:T(8,128)(2,1)}, bf16[256,1280]{1,0:T(8,128)(2,1)}) custom-call(s32[64]{0:T(128)} %lens_ref.3, f32[64,640]{1,0:T(8,128)} %get-tuple-element.9.kn_ref, f32[64,640]{1,0:T(8,128)} %get-tuple-element.10.vn_ref, bf16[256,1280]{1,0:T(8,128)(2,1)} %get-tuple-element.11.h_ref, ...), custom_call_target="tpu_custom_call" | custom-call | tf_op jit(solution)/shard_map/update/pallas_call | solution.py:502

commit v4 on v3

v4 whole, which is shorter than its diff:
```python
import functools

import jax
import jax.numpy as jnp
from jax import lax
from jax.experimental import pallas as pl
from jax.experimental.pallas import tpu as pltpu
from jax.sharding import PartitionSpec as P

EPS = 1e-6
F32 = jnp.float32
BF16 = jnp.bfloat16
MESH = pl.DeviceIdType.MESH
VMEM_LIMIT = 63 * 2 ** 20
BATCHES = 2
UPDATE_CHUNKS = 8
PARTS = 3


def remote(src, dst, send, recv, axis, index):
    return pltpu.make_async_remote_copy(
        src_ref=src, dst_ref=dst, send_sem=send, recv_sem=recv, device_id={axis: index}, device_id_type=MESH)


def entry_barrier(peers):
    barrier = pltpu.get_barrier_semaphore()
    for axis, index in peers:
        pl.semaphore_signal(barrier, inc=1, device_id={axis: index}, device_id_type=MESH)
    return lambda: pl.semaphore_wait(barrier, len(peers))


def column_to_row(col):
    rows = col.shape[0]
    return jnp.concatenate(
        [jnp.broadcast_to(col[i:i + 128], (128, 128)).T[:8] for i in range(0, rows, 128)], axis=1)


def row_to_column(row):
    rows = row.shape[1]
    return jnp.concatenate(
        [jnp.broadcast_to(row[:1, i:i + 128], (128, 128)).T for i in range(0, rows, 128)], axis=0)


def scale_rows(x, scale, gain):
    width = x.shape[1]
    cols = [x[:, i:i + 128] * scale * gain[:, i:i + 128] for i in range(0, width, 128)]
    return jnp.concatenate(cols, axis=1).astype(BF16)


def layer_kernel(nd, nx, width_full, lens_hbm, h_hbm, g1_hbm, g2_hbm, cos_hbm, sin_hbm, wq_hbm, wk_hbm, wv_hbm, wo_hbm, wg_hbm, wu_hbm, wd_hbm,
                 kc_hbm, vc_hbm, out_ref, k_out, v_out, lens_smem,
                 h_ref, g1_ref, g2_ref, cos_ref, sin_ref, wqkv, wo, wg, wu, wd, kc, vc,
                 x_buf, part, ss_send, ss_recv, a_recv, b_recv, c_send, c_recv, cos2, sin2, q_buf, o_own,
                 o_all, full, d2d_recv, xs_recv, h1_all, st_col, st_send, st_recv, sc_send, sc_recv, x2_all,
                 gu, ga_recv, gb_recv, gc_send, gc_recv, m_all, h_all,
                 w_sem, ss_s, ss_r, a_s, a_r, b_s, b_r, c_s, c_r, o_s, o_r, d_s, d_r, xs_s, xs_r,
                 st_s, st_r, sc_s, sc_r, ag_s, ag_r, agd_s, agd_r, ga_s, ga_r, gb_s, gb_r, gc_s, gc_r, m_s, m_r, mf_s, mf_r):
    dm, tp = lax.axis_index('dm'), lax.axis_index('tp')
    nxt, prv, far = lax.rem(dm + 1, nd), lax.rem(dm + nd - 1, nd), lax.rem(dm + 2, nd)
    core, xi = lax.rem(tp, 2), tp // 2
    xn, xp, xf = lax.rem(xi + 1, nx), lax.rem(xi + nx - 1, nx), lax.rem(xi + 2, nx)
    partner = tp + 1 - 2 * core
    ypeers, yall = (nxt, prv), (far, nxt, prv)
    xall = (xf, xn, xp)
    xids = tuple(2 * x + core for x in xall)
    source = (0, 2, 1)
    batch, width = h_ref.shape
    heads, slots, head = kc.shape[1:]
    rows = batch // nd
    rb = rows // BATCHES
    rh = rb // 2
    brows = nd * rb
    share = brows // (2 * nx)
    sh = share // 2
    cols = wd.shape[0]
    own_cols = cols // nd
    pc = own_cols // PARTS
    ph = pc // 2
    sends = []

    def go(*args):
        sends.append(remote(*args))
        sends[-1].start()

    def got(ref, send, recv, axis, index):
        remote(ref, ref, send, recv, axis, index).wait_recv()

    def al(x, n):
        return pl.multiple_of(x, n)

    wait_barrier = entry_barrier([('dm', y) for y in yall] + [('tp', lax.rem(tp + i, 2 * nx)) for i in range(1, 2 * nx)])
    pairs = ((h_hbm, h_ref), (wq_hbm, wqkv.at[0]), (wk_hbm, wqkv.at[1]), (wv_hbm, wqkv.at[2]), (g1_hbm, g1_ref), (cos_hbm, cos_ref), (sin_hbm, sin_ref),
             (kc_hbm, kc), (vc_hbm, vc), (wo_hbm, wo), (g2_hbm, g2_ref), (wg_hbm, wg), (wu_hbm, wu), (wd_hbm, wd))
    loads = [pltpu.make_async_copy(src, dst, w_sem.at[i]) for i, (src, dst) in enumerate(pairs)]
    loads[0].start()
    for load in loads[4:7]:
        load.start()
    loads[0].wait()
    for load in loads[1:4]:
        load.start()
    lens_load = pltpu.make_async_copy(lens_hbm, lens_smem, w_sem.at[14])
    lens_load.start()
    st_col[...] = jnp.zeros_like(st_col)
    x = h_ref[...].astype(F32)
    ss_send[...] = column_to_row(jnp.sum(x * x, axis=-1, keepdims=True))
    wait_barrier()
    for i, peer in enumerate((nxt, prv, far)):
        go(ss_send, ss_recv.at[i], ss_s.at[i], ss_r.at[i], 'dm', peer)
    for load in loads[4:7]:
        load.wait()
    hd = cos_ref.shape[1]
    cos2[:, :hd] = cos_ref[...]
    cos2[:, hd:] = cos_ref[...]
    sin2[:, :hd] = -sin_ref[...]
    sin2[:, hd:] = sin_ref[...]
    for i, peer in enumerate((nxt, prv, far)):
        got(ss_recv.at[i], ss_s.at[i], ss_r.at[i], 'dm', peer)
    for load in loads[7:]:
        load.start()
    total = ss_send[...] + ss_recv[0] + ss_recv[1] + ss_recv[2]
    scale = row_to_column(lax.rsqrt(total / width_full + EPS))
    x_buf[...] = scale_rows(h_ref[...].astype(F32), scale, g1_ref[...].astype(F32)[None, :])

    def prow(owner, b, s):
        return pl.ds(al(owner * rows + b * rb + s * rh, rh), rh)

    def qkv_a(b, t):
        for d in range(2):
            go(part.at[t, prow(far, b, d)], a_recv.at[b, d, t], a_s.at[b, d, t], a_r.at[b, d, t], 'dm', ypeers[d])

    def qkv_b(b, t):
        for d in range(2):
            go(part.at[t, prow(ypeers[d], b, 1 - d)], b_recv.at[b, d, t], b_s.at[b, d, t], b_r.at[b, d, t], 'dm', ypeers[d])

    def qkv_c(b, t):
        for d in range(2):
            got(a_recv.at[b, d, t], a_s.at[b, d, t], a_r.at[b, d, t], 'dm', ypeers[d])
            c_send[b, d, t] = a_recv[b, d, t] + part[t, prow(ypeers[d], b, d)]
            go(c_send.at[b, d, t], c_recv.at[b, d, t], c_s.at[b, d, t], c_r.at[b, d, t], 'dm', ypeers[d])

    def totals(b):
        for t, out in enumerate((q_buf, k_out, v_out)):
            for d in range(2):
                got(b_recv.at[b, d, t], b_s.at[b, d, t], b_r.at[b, d, t], 'dm', ypeers[d])
                got(c_recv.at[b, d, t], c_s.at[b, d, t], c_r.at[b, d, t], 'dm', ypeers[d])
            for d in range(2):
                tot = part[t, prow(dm, b, d)] + c_recv[b, d, t] + b_recv[b, 1 - d, t]
                here = slice(b * rb + d * rh, b * rb + (d + 1) * rh)
                for i in range(heads):
                    y = tot[:, i * head:(i + 1) * head]
                    if t < 2:
                        y = y * cos2[here] + pltpu.roll(y, head // 2, 1) * sin2[here]
                    out[here, i * head:(i + 1) * head] = y.astype(BF16).astype(F32)

    span = heads * slots
    group = 8

    def attention(lo, hi):
        lane = lax.broadcasted_iota(jnp.int32, (8, span), 1)
        lane_slot = lane % slots
        own_head = (lane // slots) == lax.broadcasted_iota(jnp.int32, (8, span), 0)
        head_row = lax.broadcasted_iota(jnp.int32, (8, head), 0)

        def body(g, carry):
            first = al(g * group, group)
            vals = [ref[pl.ds(first, group), :] for ref in (q_buf, k_out, v_out)]

            def per_head(val, r):
                y = jnp.zeros((8, head), F32)
                for i in range(heads):
                    y = jnp.where(head_row == i, jnp.broadcast_to(val[r:r + 1, i * head:(i + 1) * head], (8, head)), y)
                return y

            scores, masks, news = [], [], []
            for r in range(group):
                q = per_head(vals[0], r)
                k = kc[first + r].reshape(span, head)
                s = lax.dot_general(q.astype(BF16), k, (((1,), (1,)), ((), ())), preferred_element_type=F32)
                masks.append(own_head & (lane_slot < lens_smem[first + r]))
                scores.append(jnp.where(masks[r], s * (head ** -0.5), float(jnp.finfo(F32).min)))
                news.append(jnp.sum(q * per_head(vals[1], r), axis=-1, keepdims=True) * (head ** -0.5))
            s, new = jnp.stack(scores), jnp.stack(news)
            top = jnp.maximum(jnp.max(s, axis=-1, keepdims=True), new)
            p = jnp.where(jnp.stack(masks), jnp.exp(s - top), 0.0)
            p_new = jnp.exp(new - top)
            den = jnp.sum(p, axis=-1, keepdims=True) + p_new
            p = (p / den).astype(BF16)
            p_new = (p_new / den).astype(BF16).astype(F32)
            for r in range(group):
                o = jnp.dot(p[r], vc[first + r].reshape(span, head), preferred_element_type=F32) + p_new[r] * per_head(vals[2], r)
                for i in range(heads):
                    o_own[g, r:r + 1, i * head:(i + 1) * head] = o[i:i + 1]
            return carry

        lax.fori_loop(lo, hi, body, 0)

    def orow(owner, s=0, n=rb):
        return pl.ds(al(owner * rb + s, 16), n)

    def o_send(b):
        o_all[b, orow(dm)] = o_own[b * rb // group:(b + 1) * rb // group].reshape(rb, heads * head).astype(BF16)
        mine = o_all.at[b, orow(dm)]
        for k, peer in enumerate(yall):
            go(mine, mine, o_s.at[b, k], o_r.at[b, k], 'dm', peer)

    def o_done(b):
        for k, peer in enumerate(yall):
            got(o_all.at[b, orow(yall[source[k]])], o_s.at[b, k], o_r.at[b, k], 'dm', peer)

    def trow(owner, c, s=0, n=share):
        return pl.ds(al(c * (brows // 2) + owner * share + s, sh), n)

    order = (xf, xn, xp, xi)

    def xs_pair(u, b):
        for i, owner in enumerate(order):
            go(full.at[u, b, trow(owner, 1 - core)], d2d_recv.at[u, b, i], d_s.at[u, b, i], d_r.at[u, b, i], 'tp', partner)

    def xs_ab(u, b):
        for i, owner in enumerate(order):
            got(d2d_recv.at[u, b, i], d_s.at[u, b, i], d_r.at[u, b, i], 'tp', partner)
            here = trow(owner, core)
            full[u, b, here] = full[u, b, here] + d2d_recv[u, b, i]
            if i < 3:
                go(full.at[u, b, here], xs_recv.at[u, b, i], xs_s.at[u, b, i], xs_r.at[u, b, i], 'tp', xids[i])

    def xs_done(u, b):
        for i in range(3):
            got(xs_recv.at[u, b, i], xs_s.at[u, b, i], xs_r.at[u, b, i], 'tp', xids[i])
        return (full[u, b, trow(xi, core)] + xs_recv[u, b, 0]) + (xs_recv[u, b, 1] + xs_recv[u, b, 2])

    def ag_send(u, buf, b):
        mine = buf.at[b, trow(xi, core)]
        for k in range(3):
            go(mine, mine, ag_s.at[u, b, k], ag_r.at[u, b, k], 'tp', xids[k])
        go(mine, mine, agd_s.at[u, b, 3], agd_r.at[u, b, 3], 'tp', partner)

    def ag_fwd(u, buf, b):
        for k in (1, 2, 0):
            came = buf.at[b, trow(xall[source[k]], core)]
            got(came, ag_s.at[u, b, k], ag_r.at[u, b, k], 'tp', xids[k])
            go(came, came, agd_s.at[u, b, k], agd_r.at[u, b, k], 'tp', partner)

    def ag_done(u, buf, b):
        for k in range(3):
            got(buf.at[b, trow(xall[source[k]], 1 - core)], agd_s.at[u, b, k], agd_r.at[u, b, k], 'tp', partner)
        got(buf.at[b, trow(xi, 1 - core)], agd_s.at[u, b, 3], agd_r.at[u, b, 3], 'tp', partner)

    step = 256

    def o_proj(b):
        o_done(b)
        need(9)
        for n in range(0, width, step):
            full[0, b, :, n:n + step] = jnp.dot(o_all[b], wo[:, n:n + step], preferred_element_type=F32)
        xs_pair(0, b)

    def norm_send(b):
        attn = xs_done(0, b)
        first = trow(xi, core).start
        owner = first // rb
        here = pl.ds(al(owner * rows + b * rb + (first - owner * rb), share), share)
        h1 = h_ref[here] + attn.astype(BF16)
        h1_all[b, trow(xi, core)] = h1
        ag_send(0, h1_all, b)
        h1 = h1.astype(F32)
        col = jnp.sum(h1 * h1, axis=-1, keepdims=True)
        st_col[b, trow(xi, core)] = jnp.broadcast_to(col, (share, 128))
        st_send[b] = st_col[b].T[:8]
        for k, peer in enumerate(yall):
            go(st_send.at[b], st_recv.at[b, k], st_s.at[b, k], st_r.at[b, k], 'dm', peer)

    def norm_mid(b):
        for k, peer in enumerate(yall):
            got(st_recv.at[b, k], st_s.at[b, k], st_r.at[b, k], 'dm', peer)
        sc_send[b] = st_send[b] + st_recv[b, 0] + st_recv[b, 1] + st_recv[b, 2]
        for i in range(2 * nx - 1):
            go(sc_send.at[b], sc_recv.at[b, i], sc_s.at[b, i], sc_r.at[b, i], 'tp', lax.rem(tp + i + 1, 2 * nx))

    def norm_done(b):
        total = sc_send[b]
        for i in range(2 * nx - 1):
            got(sc_recv.at[b, i], sc_s.at[b, i], sc_r.at[b, i], 'tp', lax.rem(tp + i + 1, 2 * nx))
            total = total + sc_recv[b, i]
        ag_done(0, h1_all, b)
        need(10)
        scale = row_to_column(lax.rsqrt(total / width_full + EPS))
        x2_all[b] = scale_rows(h1_all[b].astype(F32), scale, g2_ref[...].astype(F32)[None, :])

    def columns(owner):
        return pl.ds(al(owner * own_cols, 16), own_cols)

    def gu_part(b, i):
        need(11, 12)
        for j, w in enumerate((wg, wu)):
            y = lax.dot_general(w[columns((far, nxt, prv, dm)[i])], x2_all[b], (((1,), (1,)), ((), ())), preferred_element_type=F32)
            for p in range(PARTS):
                for s in range(2):
                    gu[b, i, p, s, j] = y[p * pc + s * ph:p * pc + (s + 1) * ph]
        for p in range(PARTS):
            if i == 0:
                for d in range(2):
                    go(gu.at[b, 0, p, d], ga_recv.at[b, d, p], ga_s.at[b, d, p], ga_r.at[b, d, p], 'dm', ypeers[d])
            elif i < 3:
                d = i - 1
                go(gu.at[b, i, p, 1 - d], gb_recv.at[b, d, p], gb_s.at[b, d, p], gb_r.at[b, d, p], 'dm', ypeers[d])

    def gu_c(b, p):
        for d in range(2):
            got(ga_recv.at[b, d, p], ga_s.at[b, d, p], ga_r.at[b, d, p], 'dm', ypeers[d])
            gc_send[b, d, p] = ga_recv[b, d, p] + gu[b, 1 + d, p, d]
            go(gc_send.at[b, d, p], gc_recv.at[b, d, p], gc_s.at[b, d, p], gc_r.at[b, d, p], 'dm', ypeers[d])

    cut = (pc // 2 + 15) // 16 * 16
    cuts = ((0, cut), (cut, pc - cut))

    def mrow(owner, p, s=0, n=pc):
        return pl.ds(al(owner * own_cols + p * pc + s, 16), n)

    def straight(b):
        return b == BATCHES - 1

    def m_send(b, p):
        for d in range(2):
            got(gb_recv.at[b, d, p], gb_s.at[b, d, p], gb_r.at[b, d, p], 'dm', ypeers[d])
            got(gc_recv.at[b, d, p], gc_s.at[b, d, p], gc_r.at[b, d, p], 'dm', ypeers[d])
        halves = []
        for d in range(2):
            gate, up = (gu[b, 3, p, d, j] + gc_recv[b, d, p, j] + gb_recv[b, 1 - d, p, j] for j in range(2))
            halves.append(gate * jax.nn.sigmoid(gate) * up)
        m_all[b, mrow(dm, p)] = jnp.concatenate(halves, axis=0).astype(BF16)
        mine = m_all.at[b, mrow(dm, p)]
        if straight(b):
            go(mine, mine, mf_s.at[b, 0, p], mf_r.at[b, 0, p], 'dm', far)
        for d in range(2):
            go(mine, mine, m_s.at[b, d, p], m_r.at[b, d, p], 'dm', ypeers[d])

    def m_fwd(b, p):
        for d in range(2):
            got(m_all.at[b, mrow(ypeers[1 - d], p)], m_s.at[b, d, p], m_r.at[b, d, p], 'dm', ypeers[d])
            if not straight(b):
                piece = m_all.at[b, mrow(ypeers[1 - d], p, *cuts[d])]
                go(piece, piece, mf_s.at[b, d, p], mf_r.at[b, d, p], 'dm', ypeers[d])

    def m_done(b):
        for p in range(PARTS):
            if straight(b):
                got(m_all.at[b, mrow(far, p)], mf_s.at[b, 0, p], mf_r.at[b, 0, p], 'dm', far)
            else:
                for d in range(2):
                    got(m_all.at[b, mrow(far, p, *cuts[d])], mf_s.at[b, d, p], mf_r.at[b, d, p], 'dm', ypeers[d])

    def down(b):
        m_done(b)
        need(13)
        for n in range(0, width, step):
            full[1, b, :, n:n + step] = lax.dot_general(m_all[b], wd[:, n:n + step], (((0,), (0,)), ((), ())), preferred_element_type=F32)
        xs_pair(1, b)

    def h_send(b):
        mlp = xs_done(1, b)
        h_all[b, trow(xi, core)] = h1_all[b, trow(xi, core)] + mlp.astype(BF16)
        ag_send(1, h_all, b)

    def h_done(b):
        ag_done(1, h_all, b)
        for owner in range(nd):
            out_ref[owner * rows + b * rb:owner * rows + (b + 1) * rb] = h_all[b, owner * rb:(owner + 1) * rb]

    waited = set()

    def need(*which):
        for i in which:
            if i not in waited:
                waited.add(i)
                loads[i].wait()

    def mm(t):
        need(1 + t)
        for i in range(heads):
            part[t, :, i * head:(i + 1) * head] = jnp.dot(x_buf[...], wqkv[t, i], preferred_element_type=F32)

    mm(0)
    qkv_a(0, 0)
    qkv_b(0, 0)
    mm(1)
    mm(2)
    qkv_a(0, 1)
    qkv_a(0, 2)
    qkv_a(1, 0)
    qkv_b(0, 2)
    qkv_b(0, 1)
    qkv_a(1, 1)
    qkv_c(0, 0)
    qkv_a(1, 2)
    qkv_c(0, 1)
    qkv_c(0, 2)
    qkv_c(1, 0)
    qkv_b(1, 0)
    qkv_c(1, 1)
    qkv_b(1, 2)
    qkv_c(1, 2)
    qkv_b(1, 1)
    totals(0)
    need(7, 8)
    lens_load.wait()
    attention(2, 4)
    attention(0, 2)
    o_send(0)
    totals(1)
    attention(6, 8)
    attention(4, 6)
    o_send(1)
    o_proj(0)
    xs_ab(0, 0)
    o_proj(1)
    xs_ab(0, 1)
    norm_send(0)
    norm_mid(0)
    norm_send(1)
    ag_fwd(0, h1_all, 0)
    norm_done(0)
    gu_part(0, 0)
    norm_mid(1)
    ag_fwd(0, h1_all, 1)
    gu_part(0, 1)
    norm_done(1)
    gu_part(1, 0)
    gu_part(0, 2)
    gu_part(0, 3)
    gu_c(0, 0)
    gu_c(0, 1)
    gu_c(0, 2)
    gu_part(1, 1)
    m_send(0, 0)
    m_send(0, 1)
    m_send(0, 2)
    gu_part(1, 2)
    gu_part(1, 3)
    gu_c(1, 1)
    gu_c(1, 2)
    gu_c(1, 0)
    m_fwd(0, 0)
    m_fwd(0, 1)
    m_fwd(0, 2)
    m_send(1, 1)
    m_send(1, 2)
    m_send(1, 0)
    down(0)
    m_fwd(1, 1)
    xs_ab(1, 0)
    m_fwd(1, 2)
    m_fwd(1, 0)
    down(1)
    xs_ab(1, 1)
    h_send(0)
    h_send(1)
    ag_fwd(1, h_all, 0)
    h_done(0)
    ag_fwd(1, h_all, 1)
    h_done(1)
    for copy in sends:
        copy.wait_send()


def layer(nd, nx, lens, hidden, g1, g2, cos, sin, wq, wk, wv, wo, wg, wu, wd, kc, vc):
    batch, width = hidden.shape
    heads, _, head = wq.shape
    rows, inner, cols = batch // nd, heads * head, wd.shape[0]
    nb = BATCHES
    rh = rows // nb // 2
    brows = batch // nb
    share = brows // (2 * nx)
    vmem = pl.BlockSpec(memory_space=pltpu.VMEM)
    hbm = pl.BlockSpec(memory_space=pl.ANY)
    vm = pltpu.VMEM
    dma = pltpu.SemaphoreType.DMA
    piece = vm((nb, 2, 3, rh, inner), F32)
    ph = cols // nd // PARTS // 2
    gpiece = vm((nb, 2, PARTS, 2, ph, brows), F32)
    return pl.pallas_call(
        functools.partial(layer_kernel, nd, nx, width * nd),
        out_shape=[jax.ShapeDtypeStruct((batch, width), BF16), jax.ShapeDtypeStruct((rows, inner), F32), jax.ShapeDtypeStruct((rows, inner), F32)],
        in_specs=[hbm] * 15,
        out_specs=[vmem] * 3,
        scratch_shapes=[
            pltpu.SMEM(lens.shape, jnp.int32), vm(hidden.shape, BF16), vm(g1.shape, BF16), vm(g2.shape, BF16), vm(cos.shape, F32), vm(sin.shape, F32),
            vm((3, heads, width, head), BF16), vm(wo.shape, BF16), vm(wg.shape, BF16), vm(wu.shape, BF16), vm(wd.shape, BF16),
            vm(kc.shape, BF16), vm(vc.shape, BF16),
            vm((batch, width), BF16), vm((3, batch, inner), F32), vm((8, batch), F32), vm((3, 8, batch), F32),
            piece, piece, piece, piece, vm((rows, head), F32), vm((rows, head), F32), vm((rows, inner), F32), vm((rows // 8, 8, inner), F32),
            vm((nb, brows, inner), BF16), vm((2, nb, brows, width), F32), vm((2, nb, nx, share, width), F32),
            vm((2, nb, 3, share, width), F32), vm((nb, brows, width), BF16), vm((nb, brows, 128), F32), vm((nb, 8, brows), F32), vm((nb, 3, 8, brows), F32),
            vm((nb, 8, brows), F32), vm((nb, 2 * nx - 1, 8, brows), F32), vm((nb, brows, width), BF16),
            vm((nb, 4, PARTS, 2, 2, ph, brows), F32), gpiece, gpiece, gpiece, gpiece, vm((nb, cols, brows), BF16), vm((nb, brows, width), BF16),
            dma((15,)), dma((3,)), dma((3,))] + [dma((nb, 2, 3))] * 6 + [dma((nb, 3))] * 2 + [dma((2, nb, nx))] * 2 + [dma((2, nb, 3))] * 2
        + [dma((nb, 3))] * 2 + [dma((nb, 2 * nx - 1))] * 2 + [dma((2, nb, 3))] * 2 + [dma((2, nb, nx))] * 2 + [dma((nb, 2, PARTS))] * 10,
        compiler_params=pltpu.CompilerParams(collective_id=0, has_side_effects=True, vmem_limit_bytes=VMEM_LIMIT),
        name='layer',
    )(lens, hidden, g1, g2, cos, sin, wq, wk, wv, wo, wg, wu, wd, kc, vc)


def update_kernel(lens_ref, kn_ref, vn_ref, h_hbm, kc_hbm, vc_hbm, ko_hbm, vo_hbm, out_hbm, kc, vc, h_buf, in_sem, out_sem):
    rows, heads, slots, head = kc.shape
    chunk = rows // UPDATE_CHUNKS
    window = 16
    pos = lax.broadcasted_iota(jnp.int32, (heads, window, head), 1)

    def copies(c):
        here = pl.ds(c * chunk, chunk)
        return [(pltpu.make_async_copy(src.at[here], buf.at[here], in_sem.at[i, c]), pltpu.make_async_copy(buf.at[here], dst.at[here], out_sem.at[i, c]))
                for i, (src, buf, dst) in enumerate(((kc_hbm, kc, ko_hbm), (vc_hbm, vc, vo_hbm)))]

    h_in = pltpu.make_async_copy(h_hbm, h_buf, in_sem.at[2, 0])
    h_out = pltpu.make_async_copy(h_buf, out_hbm, out_sem.at[2, 0])
    for c in range(UPDATE_CHUNKS):
        for load, _ in copies(c):
            load.start()
    h_in.start()

    def body(c, carry):
        pairs = copies(c)
        for load, _ in pairs:
            load.wait()
        first = pl.multiple_of(c * chunk, chunk)
        new_all = [ref[pl.ds(first, chunk), :] for ref in (kn_ref, vn_ref)]
        for r in range(chunk):
            length = lens_ref[first + r]
            base = pl.multiple_of(length // window * window, window)
            write = pos == length - base
            for vals, buf in zip(new_all, (kc, vc)):
                new = jnp.stack([jnp.broadcast_to(vals[r:r + 1, i * head:(i + 1) * head], (window, head)) for i in range(heads)])
                old = buf[first + r, :, pl.ds(base, window), :]
                buf[first + r, :, pl.ds(base, window), :] = jnp.where(write, new, old.astype(F32)).astype(BF16)
        for _, store in pairs:
            store.start()
        return carry

    lax.fori_loop(0, UPDATE_CHUNKS, body, 0)
    h_in.wait()
    h_out.start()
    for c in range(UPDATE_CHUNKS):
        for _, store in copies(c):
            store.wait()
    h_out.wait()


def update(lens, kn, vn, h, kc, vc):
    smem = pl.BlockSpec(memory_space=pltpu.SMEM)
    vmem = pl.BlockSpec(memory_space=pltpu.VMEM)
    hbm = pl.BlockSpec(memory_space=pl.ANY)
    dma = pltpu.SemaphoreType.DMA
    return pl.pallas_call(
        update_kernel,
        in_specs=[smem, vmem, vmem, hbm, hbm, hbm],
        out_specs=[hbm] * 3,
        out_shape=[jax.ShapeDtypeStruct(kc.shape, BF16), jax.ShapeDtypeStruct(vc.shape, BF16), jax.ShapeDtypeStruct(h.shape, BF16)],
        scratch_shapes=[pltpu.VMEM(kc.shape, BF16), pltpu.VMEM(vc.shape, BF16), pltpu.VMEM(h.shape, BF16),
                        dma((3, UPDATE_CHUNKS)), dma((3, UPDATE_CHUNKS))],
        compiler_params=pltpu.CompilerParams(vmem_limit_bytes=VMEM_LIMIT),
        name='update',
    )(lens, kn, vn, h, kc, vc)


def solution(mesh):
    nd, nx = mesh.shape['dm'], mesh.shape['tp'] // 2
    row_spec = P('dp', 'dm')
    cache_spec = P(('dp', 'dm'), None, 'tp', None)
    batch_spec = P(('dp', 'dm'))
    rope_spec = P(('dp', 'dm'), None)
    in_specs = (row_spec, P('dm', 'tp', None), P('dm', 'tp', None), P('dm', 'tp', None), P('tp', None, 'dm'), P('dm', 'tp'), P('dm', 'tp'), P('tp', 'dm'), P('dm'), P('dm'), cache_spec, cache_spec, batch_spec, rope_spec, rope_spec)
    out_specs = (row_spec, cache_spec, cache_spec)

    def local_layer(hidden, w_q, w_k, w_v, w_o, w_gate, w_up, w_down, norm_attn, norm_mlp, k_cache, v_cache, seq_lens, rope_cos, rope_sin):
        wq, wk, wv = (w.transpose(1, 0, 2) for w in (w_q, w_k, w_v))
        kc, vc = (c.transpose(0, 2, 1, 3) for c in (k_cache, v_cache))
        h_out, kn, vn = layer(nd, nx, seq_lens, hidden, norm_attn, norm_mlp, rope_cos, rope_sin, wq, wk, wv, w_o.reshape(-1, w_o.shape[-1]), w_gate.T, w_up.T, w_down, kc, vc)
        ko, vo, h_out = update(seq_lens, kn, vn, h_out, kc, vc)
        return h_out, ko.transpose(0, 2, 1, 3), vo.transpose(0, 2, 1, 3)

    return jax.shard_map(local_layer, mesh=mesh, in_specs=in_specs, out_specs=out_specs, check_vma=False)
```

time: 141 us -> 118 us (0.84)
  Pallas kernels: 140 us -> 117 us
    pallas_call x1, Pallas kernels: 129 us -> 107 us  [layer(): pl.pallas_call(functools.partial(layer_kernel, nd, nx, width * nd), out_s...]
    pallas_call x1, Pallas kernels: 11.4 us -> 9.55 us  [update(): pl.pallas_call(update_kernel, in_specs=[smem, vmem, vmem, hbm, hbm, hbm],...]
where the time goes in v4:
time: 118 us; the launch traced here: 117 us
  Pallas kernels  117 us (99%)
    pallas_call x1, Pallas kernels, layer(): pl.pallas_call(functools.partial(layer_kernel, nd, nx, width * nd), out_s...  107 us
    pallas_call x1, Pallas kernels, update(): pl.pallas_call(update_kernel, in_specs=[smem, vmem, vmem, hbm, hbm, hbm],...  9.55 us

profile of v4, /device:TPU:97, one launch (start us, length us, event | category | flops | bytes accessed | tf_op | source)
XLA Modules:
  0.0 117.5 jit_solution(7765527903639729678)
XLA Ops:
  0.6 107.1 %layer.1 = (bf16[256,1280]{1,0:T(8,128)(2,1)}, f32[64,640]{1,0:T(8,128)}, f32[64,640]{1,0:T(8,128)}) custom-call(s32[64]{0:T(128)} %lens_ref.1, bf16[256,1280]{1,0:T(8,128)(2,1)} %h_hbm.1, bf16[1280]{0:T(1024)(128)(2,1)} %g1_hbm.1, bf16[1280]{0:T(1024)(128)(2,1)} %g2_hbm.1, f32[64,64]{1,0:T(8,128)} %cos_hbm.1, f32[64,64]{1,0:T(8,128)} %sin_hbm.1, ...), custom_call_target="tpu_custom_call" | custom-call | tf_op jit(solution)/shard_map/layer/pallas_call | solution.py:481
  107.8 9.6 %update.1 = (bf16[64,5,64,128]{3,2,1,0:T(8,128)(2,1)}, bf16[64,5,64,128]{3,2,1,0:T(8,128)(2,1)}, bf16[256,1280]{1,0:T(8,128)(2,1)}) custom-call(s32[64]{0:T(128)} %lens_ref.1, f32[64,640]{1,0:T(8,128)} %get-tuple-element.9.kn_ref, f32[64,640]{1,0:T(8,128)} %get-tuple-element.10.vn_ref, bf16[256,1280]{1,0:T(8,128)(2,1)} %get-tuple-element.11.h_hbm, ...), custom_call_target="tpu_custom_call" | custom-call | tf_op jit(solution)/shard_map/update/pallas_call | solution.py:553

commit v5 on v4

--- a/solution.py
+++ b/solution.py
@@ -11,7 +11,8 @@
 F32 = jnp.float32
 BF16 = jnp.bfloat16
 MESH = pl.DeviceIdType.MESH
-VMEM_LIMIT = 63 * 2 ** 20
+LAYER_VMEM = 52 * 2 ** 20
+UPDATE_VMEM = 16 * 2 ** 20
 BATCHES = 2
 UPDATE_CHUNKS = 8
 PARTS = 3
@@ -48,8 +49,8 @@
 
 
 def layer_kernel(nd, nx, width_full, lens_hbm, h_hbm, g1_hbm, g2_hbm, cos_hbm, sin_hbm, wq_hbm, wk_hbm, wv_hbm, wo_hbm, wg_hbm, wu_hbm, wd_hbm,
-                 kc_hbm, vc_hbm, out_ref, k_out, v_out, lens_smem,
-                 h_ref, g1_ref, g2_ref, cos_ref, sin_ref, wqkv, wo, wg, wu, wd, kc, vc,
+                 kc_hbm, vc_hbm, out_ref, k_out, v_out, kc, vc, lens_smem,
+                 h_ref, g1_ref, g2_ref, cos_ref, sin_ref, wqkv, wo, wg, wu, wd,
                  x_buf, part, ss_send, ss_recv, a_recv, b_recv, c_send, c_recv, cos2, sin2, q_buf, o_own,
                  o_all, full, d2d_recv, xs_recv, h1_all, st_col, st_send, st_recv, sc_send, sc_recv, x2_all,
                  gu, ga_recv, gb_recv, gc_send, gc_recv, m_all, h_all,
@@ -480,13 +481,12 @@
     gpiece = vm((nb, 2, PARTS, 2, ph, brows), F32)
     return pl.pallas_call(
         functools.partial(layer_kernel, nd, nx, width * nd),
-        out_shape=[jax.ShapeDtypeStruct((batch, width), BF16), jax.ShapeDtypeStruct((rows, inner), F32), jax.ShapeDtypeStruct((rows, inner), F32)],
+        out_shape=[vm((batch, width), BF16), vm((rows, inner), F32), vm((rows, inner), F32), vm(kc.shape, BF16), vm(vc.shape, BF16)],
         in_specs=[hbm] * 15,
-        out_specs=[vmem] * 3,
+        out_specs=[vmem] * 5,
         scratch_shapes=[
             pltpu.SMEM(lens.shape, jnp.int32), vm(hidden.shape, BF16), vm(g1.shape, BF16), vm(g2.shape, BF16), vm(cos.shape, F32), vm(sin.shape, F32),
             vm((3, heads, width, head), BF16), vm(wo.shape, BF16), vm(wg.shape, BF16), vm(wu.shape, BF16), vm(wd.shape, BF16),
-            vm(kc.shape, BF16), vm(vc.shape, BF16),
             vm((batch, width), BF16), vm((3, batch, inner), F32), vm((8, batch), F32), vm((3, 8, batch), F32),
             piece, piece, piece, piece, vm((rows, head), F32), vm((rows, head), F32), vm((rows, inner), F32), vm((rows // 8, 8, inner), F32),
             vm((nb, brows, inner), BF16), vm((2, nb, brows, width), F32), vm((2, nb, nx, share, width), F32),
@@ -495,71 +495,78 @@
             vm((nb, 4, PARTS, 2, 2, ph, brows), F32), gpiece, gpiece, gpiece, gpiece, vm((nb, cols, brows), BF16), vm((nb, brows, width), BF16),
             dma((15,)), dma((3,)), dma((3,))] + [dma((nb, 2, 3))] * 6 + [dma((nb, 3))] * 2 + [dma((2, nb, nx))] * 2 + [dma((2, nb, 3))] * 2
         + [dma((nb, 3))] * 2 + [dma((nb, 2 * nx - 1))] * 2 + [dma((2, nb, 3))] * 2 + [dma((2, nb, nx))] * 2 + [dma((nb, 2, PARTS))] * 10,
-        compiler_params=pltpu.CompilerParams(collective_id=0, has_side_effects=True, vmem_limit_bytes=VMEM_LIMIT),
+        compiler_params=pltpu.CompilerParams(collective_id=0, has_side_effects=True, vmem_limit_bytes=LAYER_VMEM),
         name='layer',
     )(lens, hidden, g1, g2, cos, sin, wq, wk, wv, wo, wg, wu, wd, kc, vc)
 
 
-def update_kernel(lens_ref, kn_ref, vn_ref, h_hbm, kc_hbm, vc_hbm, ko_hbm, vo_hbm, out_hbm, kc, vc, h_buf, in_sem, out_sem):
+def update_kernel(lens_ref, kn_ref, vn_ref, h_ref, kc, vc, ko_hbm, vo_hbm, out_hbm, k_win, v_win, bulk_sem, win_sem, h_sem):
     rows, heads, slots, head = kc.shape
     chunk = rows // UPDATE_CHUNKS
+    window = k_win.shape[2]
+    pos = lax.broadcasted_iota(jnp.int32, (heads, window, head), 1)
+    sides = ((kn_ref, kc, k_win, ko_hbm), (vn_ref, vc, v_win, vo_hbm))
+
+    def here(c):
+        return pl.ds(pl.multiple_of(c * chunk, chunk), chunk)
+
+    def bulk(i, c):
+        return pltpu.make_async_copy(sides[i][1].at[here(c)], sides[i][3].at[here(c)], bulk_sem.at[i, c])
+
+    for c in range(UPDATE_CHUNKS):
+        for i in range(2):
+            bulk(i, c).start()
+    h_copy = pltpu.make_async_copy(h_ref, out_hbm, h_sem)
+    h_copy.start()
+
+    def base_of(row):
+        return pl.multiple_of(lens_ref[row] // window * window, window)
+
+    def patch(c, carry):
+        first = pl.multiple_of(c * chunk, chunk)
+        new_all = [side[0][pl.ds(first, chunk), :] for side in sides]
+        for r in range(chunk):
+            base = base_of(first + r)
+            write = pos == lens_ref[first + r] - base
+            for vals, (_, cache, win, _) in zip(new_all, sides):
+                new = jnp.stack([jnp.broadcast_to(vals[r:r + 1, i * head:(i + 1) * head], (window, head)) for i in range(heads)])
+                win[first + r] = jnp.where(write, new, cache[first + r, :, pl.ds(base, window), :].astype(F32)).astype(BF16)
+        return carry
+
+    lax.fori_loop(0, UPDATE_CHUNKS, patch, 0)
+
+    def put(c, carry):
+        for i, (_, _, win, out) in enumerate(sides):
+            bulk(i, c).wait()
+            for r in range(chunk):
+                row = c * chunk + r
+                pltpu.make_async_copy(win.at[row], out.at[row, :, pl.ds(base_of(row), window), :], win_sem.at[i, c]).start()
+        return carry
+
+    lax.fori_loop(0, UPDATE_CHUNKS, put, 0)
+    for c in range(UPDATE_CHUNKS):
+        for i, (_, _, win, out) in enumerate(sides):
+            pltpu.make_async_copy(win.at[here(c)], out.at[here(c), :, pl.ds(0, window), :], win_sem.at[i, c]).wait()
+    h_copy.wait()
+
+
+def update(lens, kn, vn, h, kc, vc):
+    rows, heads, slots, head = kc.shape
     window = 16
-    pos = lax.broadcasted_iota(jnp.int32, (heads, window, head), 1)
-
-    def copies(c):
-        here = pl.ds(c * chunk, chunk)
-        return [(pltpu.make_async_copy(src.at[here], buf.at[here], in_sem.at[i, c]), pltpu.make_async_copy(buf.at[here], dst.at[here], out_sem.at[i, c]))
-                for i, (src, buf, dst) in enumerate(((kc_hbm, kc, ko_hbm), (vc_hbm, vc, vo_hbm)))]
-
-    h_in = pltpu.make_async_copy(h_hbm, h_buf, in_sem.at[2, 0])
-    h_out = pltpu.make_async_copy(h_buf, out_hbm, out_sem.at[2, 0])
-    for c in range(UPDATE_CHUNKS):
-        for load, _ in copies(c):
-            load.start()
-    h_in.start()
-
-    def body(c, carry):
-        pairs = copies(c)
-        for load, _ in pairs:
-            load.wait()
-        first = pl.multiple_of(c * chunk, chunk)
-        new_all = [ref[pl.ds(first, chunk), :] for ref in (kn_ref, vn_ref)]
-        for r in range(chunk):
-            length = lens_ref[first + r]
-            base = pl.multiple_of(length // window * window, window)
-            write = pos == length - base
-            for vals, buf in zip(new_all, (kc, vc)):
-                new = jnp.stack([jnp.broadcast_to(vals[r:r + 1, i * head:(i + 1) * head], (window, head)) for i in range(heads)])
-                old = buf[first + r, :, pl.ds(base, window), :]
-                buf[first + r, :, pl.ds(base, window), :] = jnp.where(write, new, old.astype(F32)).astype(BF16)
-        for _, store in pairs:
-            store.start()
-        return carry
-
-    lax.fori_loop(0, UPDATE_CHUNKS, body, 0)
-    h_in.wait()
-    h_out.start()
-    for c in range(UPDATE_CHUNKS):
-        for _, store in copies(c):
-            store.wait()
-    h_out.wait()
-
-
-def update(lens, kn, vn, h, kc, vc):
     smem = pl.BlockSpec(memory_space=pltpu.SMEM)
     vmem = pl.BlockSpec(memory_space=pltpu.VMEM)
     hbm = pl.BlockSpec(memory_space=pl.ANY)
     dma = pltpu.SemaphoreType.DMA
     return pl.pallas_call(
         update_kernel,
-        in_specs=[smem, vmem, vmem, hbm, hbm, hbm],
+        in_specs=[smem] + [vmem] * 5,
         out_specs=[hbm] * 3,
         out_shape=[jax.ShapeDtypeStruct(kc.shape, BF16), jax.ShapeDtypeStruct(vc.shape, BF16), jax.ShapeDtypeStruct(h.shape, BF16)],
-        scratch_shapes=[pltpu.VMEM(kc.shape, BF16), pltpu.VMEM(vc.shape, BF16), pltpu.VMEM(h.shape, BF16),
-                        dma((3, UPDATE_CHUNKS)), dma((3, UPDATE_CHUNKS))],
-        compiler_params=pltpu.CompilerParams(vmem_limit_bytes=VMEM_LIMIT),
+        scratch_shapes=[pltpu.VMEM((rows, heads, window, head), BF16), pltpu.VMEM((rows, heads, window, head), BF16),
+                        dma((2, UPDATE_CHUNKS)), dma((2, UPDATE_CHUNKS)), dma],
+        compiler_params=pltpu.CompilerParams(vmem_limit_bytes=UPDATE_VMEM),
         name='update',
-    )(lens, kn, vn, h, kc, vc)
+    )(lens, *(pltpu.with_memory_space_constraint(x, pltpu.VMEM) for x in (kn, vn, h, kc, vc)))
 
 
 def solution(mesh):
@@ -574,7 +581,7 @@
     def local_layer(hidden, w_q, w_k, w_v, w_o, w_gate, w_up, w_down, norm_attn, norm_mlp, k_cache, v_cache, seq_lens, rope_cos, rope_sin):
         wq, wk, wv = (w.transpose(1, 0, 2) for w in (w_q, w_k, w_v))
         kc, vc = (c.transpose(0, 2, 1, 3) for c in (k_cache, v_cache))
-        h_out, kn, vn = layer(nd, nx, seq_lens, hidden, norm_attn, norm_mlp, rope_cos, rope_sin, wq, wk, wv, w_o.reshape(-1, w_o.shape[-1]), w_gate.T, w_up.T, w_down, kc, vc)
+        h_out, kn, vn, kc, vc = layer(nd, nx, seq_lens, hidden, norm_attn, norm_mlp, rope_cos, rope_sin, wq, wk, wv, w_o.reshape(-1, w_o.shape[-1]), w_gate.T, w_up.T, w_down, kc, vc)
         ko, vo, h_out = update(seq_lens, kn, vn, h_out, kc, vc)
         return h_out, ko.transpose(0, 2, 1, 3), vo.transpose(0, 2, 1, 3)
 

time: 118 us -> 113 us (0.958)
  Pallas kernels: 117 us -> 112 us
    pallas_call x1, Pallas kernels: 9.55 us -> 5.66 us  [update(): pl.pallas_call(update_kernel, in_specs=[smem] + [vmem] * 5, out_specs=[hb...]
where the time goes in v5:
time: 113 us
  Pallas kernels  112 us (99%)
    pallas_call x1, Pallas kernels, layer(): pl.pallas_call(functools.partial(layer_kernel, nd, nx, width * nd), out_s...  106 us
    pallas_call x1, Pallas kernels, update(): pl.pallas_call(update_kernel, in_specs=[smem] + [vmem] * 5, out_specs=[hb...  5.66 us

profile of v5, /device:TPU:97, one launch (start us, length us, event | category | flops | bytes accessed | tf_op | source)
XLA Modules:
  0.0 112.6 jit_solution(4152335326448376391)
XLA Ops:
  0.6 0.0 copy-start
  0.6 106.1 %layer.1 = (bf16[256,1280]{1,0:T(8,128)(2,1)S(1)}, f32[64,640]{1,0:T(8,128)S(1)}, f32[64,640]{1,0:T(8,128)S(1)}, bf16[64,5,64,128]{3,2,1,0:T(8,128)(2,1)S(1)}, bf16[64,5,64,128]{3,2,1,0:T(8,128)(2,1)S(1)}) custom-call(s32[64]{0:T(128)} %lens_ref.1, bf16[256,1280]{1,0:T(8,128)(2,1)} %h_hbm.1, bf16[1280]{0:T(1024)(128)(2,1)} %g1_hbm.1, ...), custom_call_target="tpu_custom_call" | custom-call | tf_op jit(solution)/shard_map/layer/pallas_call | solution.py:482
  106.7 0.0 copy-done
  106.8 5.7 %update.1 = (bf16[64,5,64,128]{3,2,1,0:T(8,128)(2,1)}, bf16[64,5,64,128]{3,2,1,0:T(8,128)(2,1)}, bf16[256,1280]{1,0:T(8,128)(2,1)}) custom-call(s32[64]{0:T(128)S(1)} %copy-done, f32[64,640]{1,0:T(8,128)S(1)} %get-tuple-element.11.kn_ref, f32[64,640]{1,0:T(8,128)S(1)} %get-tuple-element.12.vn_ref, bf16[256,1280]{1,0:T(8,128)(2,1)S(1)} %get-tuple-element.13.h_ref, ...), custom_call_target="tpu_custom_call" | custom-call | tf_op jit(solution)/shard_map/update/pallas_call | solution.py:560
Async XLA Ops:
  0.6 106.1 %copy-start = (s32[64]{0:T(128)S(1)}, s32[64]{0:T(128)}, u32[]{:S(2)}) copy-start(s32[64]{0:T(128)} %lens_ref.1) | copy-start | bytes 772

commit v6 on v5

--- a/solution.py
+++ b/solution.py
@@ -385,80 +385,80 @@
     qkv_a(0, 0)
     qkv_b(0, 0)
     mm(1)
+    qkv_a(0, 1)
     mm(2)
-    qkv_a(0, 1)
     qkv_a(0, 2)
-    qkv_a(1, 0)
+    qkv_b(0, 1)
     qkv_b(0, 2)
-    qkv_b(0, 1)
-    qkv_a(1, 1)
     qkv_c(0, 0)
-    qkv_a(1, 2)
     qkv_c(0, 1)
     qkv_c(0, 2)
-    qkv_c(1, 0)
-    qkv_b(1, 0)
-    qkv_c(1, 1)
-    qkv_b(1, 2)
-    qkv_c(1, 2)
+    qkv_a(1, 0)
+    qkv_a(1, 1)
     qkv_b(1, 1)
     totals(0)
+    qkv_a(1, 2)
+    qkv_b(1, 2)
     need(7, 8)
     lens_load.wait()
+    attention(0, 2)
     attention(2, 4)
-    attention(0, 2)
     o_send(0)
+    qkv_b(1, 0)
+    qkv_c(1, 0)
+    qkv_c(1, 1)
+    o_proj(0)
+    qkv_c(1, 2)
+    xs_ab(0, 0)
     totals(1)
+    attention(4, 6)
     attention(6, 8)
-    attention(4, 6)
     o_send(1)
-    o_proj(0)
-    xs_ab(0, 0)
+    norm_send(0)
+    norm_mid(0)
     o_proj(1)
     xs_ab(0, 1)
-    norm_send(0)
-    norm_mid(0)
-    norm_send(1)
     ag_fwd(0, h1_all, 0)
     norm_done(0)
     gu_part(0, 0)
+    norm_send(1)
+    gu_part(0, 1)
+    gu_part(0, 2)
+    gu_part(0, 3)
+    ag_fwd(0, h1_all, 1)
     norm_mid(1)
-    ag_fwd(0, h1_all, 1)
-    gu_part(0, 1)
+    gu_c(0, 1)
+    gu_c(0, 2)
+    gu_c(0, 0)
     norm_done(1)
     gu_part(1, 0)
-    gu_part(0, 2)
-    gu_part(0, 3)
-    gu_c(0, 0)
-    gu_c(0, 1)
-    gu_c(0, 2)
+    m_send(0, 1)
+    m_send(0, 0)
     gu_part(1, 1)
-    m_send(0, 0)
-    m_send(0, 1)
-    m_send(0, 2)
     gu_part(1, 2)
-    gu_part(1, 3)
-    gu_c(1, 1)
-    gu_c(1, 2)
     gu_c(1, 0)
     m_fwd(0, 0)
+    m_send(0, 2)
+    gu_c(1, 1)
     m_fwd(0, 1)
+    gu_part(1, 3)
+    gu_c(1, 2)
     m_fwd(0, 2)
+    m_send(1, 0)
     m_send(1, 1)
+    m_fwd(1, 1)
     m_send(1, 2)
-    m_send(1, 0)
     down(0)
-    m_fwd(1, 1)
+    m_fwd(1, 2)
     xs_ab(1, 0)
-    m_fwd(1, 2)
     m_fwd(1, 0)
     down(1)
     xs_ab(1, 1)
     h_send(0)
     h_send(1)
     ag_fwd(1, h_all, 0)
+    ag_fwd(1, h_all, 1)
     h_done(0)
-    ag_fwd(1, h_all, 1)
     h_done(1)
     for copy in sends:
         copy.wait_send()

time: 113 us -> 112 us (level)
  no operation moved by 1% of the time
where the time goes in v6:
time: 112 us
  Pallas kernels  111 us (99%)
    pallas_call x1, Pallas kernels, layer(): pl.pallas_call(functools.partial(layer_kernel, nd, nx, width * nd), out_s...  105 us
    pallas_call x1, Pallas kernels, update(): pl.pallas_call(update_kernel, in_specs=[smem] + [vmem] * 5, out_specs=[hb...  5.66 us

profile of v6, /device:TPU:97, one launch (start us, length us, event | category | flops | bytes accessed | tf_op | source)
XLA Modules:
  0.0 111.9 jit_solution(7467839769979704727)
XLA Ops:
  0.6 0.0 copy-start
  0.6 105.4 %layer.1 = (bf16[256,1280]{1,0:T(8,128)(2,1)S(1)}, f32[64,640]{1,0:T(8,128)S(1)}, f32[64,640]{1,0:T(8,128)S(1)}, bf16[64,5,64,128]{3,2,1,0:T(8,128)(2,1)S(1)}, bf16[64,5,64,128]{3,2,1,0:T(8,128)(2,1)S(1)}) custom-call(s32[64]{0:T(128)} %lens_ref.1, bf16[256,1280]{1,0:T(8,128)(2,1)} %h_hbm.1, bf16[1280]{0:T(1024)(128)(2,1)} %g1_hbm.1, ...), custom_call_target="tpu_custom_call" | custom-call | tf_op jit(solution)/shard_map/layer/pallas_call | solution.py:482
  106.1 0.0 copy-done
  106.1 5.7 %update.1 = (bf16[64,5,64,128]{3,2,1,0:T(8,128)(2,1)}, bf16[64,5,64,128]{3,2,1,0:T(8,128)(2,1)}, bf16[256,1280]{1,0:T(8,128)(2,1)}) custom-call(s32[64]{0:T(128)S(1)} %copy-done, f32[64,640]{1,0:T(8,128)S(1)} %get-tuple-element.11.kn_ref, f32[64,640]{1,0:T(8,128)S(1)} %get-tuple-element.12.vn_ref, bf16[256,1280]{1,0:T(8,128)(2,1)S(1)} %get-tuple-element.13.h_ref, ...), custom_call_target="tpu_custom_call" | custom-call | tf_op jit(solution)/shard_map/update/pallas_call | solution.py:560
Async XLA Ops:
  0.6 105.4 %copy-start = (s32[64]{0:T(128)S(1)}, s32[64]{0:T(128)}, u32[]{:S(2)}) copy-start(s32[64]{0:T(128)} %lens_ref.1) | copy-start | bytes 772
